TPU v7x, 256 devices: a whole 4x4x8 slice. The times are simulated.
256 devices in a mesh: group: 4 (over z_hi, core), orb: 64 (over x, z_lo, y).
Axes of the slice: x: 4, y: 4, z: 8 (z_hi: 2, z_lo: 4; z = z_hi * 4 + z_lo), core: 2. Of those that a mesh axis runs over, the one named last changes fastest.
Arguments:
- orbitals: bfloat16 [96, 512, 1024], P(None, 'orb'), may hold values from -40 to 40
- potential: float32 [512, 1024], P('orb'), may hold values from -5 to 5
- box_shift: int32 [96], replicated, may hold values from 0 to 31, as said below
- pair_partner: int32 [192, 56], replicated, may hold values from -1 to 1535, as said below
- pair_member: int32 [192, 56], replicated, may hold values from 0 to 7
Outputs:
- hamiltonian: float32 [96, 512, 1024], P(None, 'orb')
Inputs may be any that keep to these rules, and one draw needn't show every extreme that they name: Exactly 24 colors have each value of box_shift // 8. `pair_partner`: -1 marks an empty slot; a live slot p of block b names a home orbital of slab (b // 3 + p // 8 - 3) mod (64); some block has every slot live.
All inputs are finite; a program needn't handle non-finite values.
Results may differ from a plain program's by a relative error of at most 0.0004.
Values may be sent and summed in bfloat16 or wider, within the bound.
A program may use at most 128 MiB of HBM per device.

v0:
```python
import functools

import jax
import jax.numpy as jnp
import numpy as np
from jax import lax
from jax.experimental import pallas as pl
from jax.experimental.pallas import tpu as pltpu
from jax.sharding import PartitionSpec as P

B = 32
CX = 8
MEMBERS = 8
NCOL = 96
HALF = NCOL // 2
SLABS = 64
WIDTH = 4
CROSS = B * B
QUAD = CROSS // 4
WIN = (WIDTH + 1) * CX
MINE = 12
BATCH = 8
SLOTS = 168

lap_weights = (
    -5369.0 / 1800.0,
    12.0 / 7.0,
    -15.0 / 56.0,
    10.0 / 189.0,
    -1.0 / 112.0,
    2.0 / 1925.0,
    -1.0 / 16632.0,
)
stencil_reach = 6
mixing = 0.25


def halves(values):
    hi = values.astype(jnp.bfloat16).astype(np.float64)
    lo = (values - hi).astype(jnp.bfloat16).astype(np.float64)
    return hi, lo


def tables():
    idx = np.arange(1, B + 1)
    sine = np.sqrt(2.0 / (B + 1)) * np.sin(np.pi * np.outer(idx, idx) / (B + 1))
    single = 2.0 - 2.0 * np.cos(np.pi * idx / (B + 1))
    part = [sine[: B // 2, p::2] for p in (0, 1)]
    lap = np.zeros((B, B))
    for o, w in enumerate(lap_weights):
        lap += w * (np.eye(B, k=o) if o == 0 else np.eye(B, k=o) + np.eye(B, k=-o))
    flip = lap[: B // 2, ::-1][:, : B // 2]
    fold = [lap[: B // 2, : B // 2] + flip, lap[: B // 2, : B // 2] - flip]
    eye = np.eye(B // 2)
    kmat, lmat, modes = [], [], []
    for py in (0, 1):
        for pz in (0, 1):
            kmat.append(np.kron(part[py], part[pz]))
            lmat.append(-0.125 * (np.kron(fold[py], eye) + np.kron(eye, fold[pz])).T)
            cross = single[py::2][:, None] + single[pz::2][None, :]
            modes.append(single[:, None] + cross.reshape(1, -1))
    inv = (-mixing / np.concatenate(modes, axis=1)).astype(np.float32)
    ktab = np.stack(halves(np.stack(kmat))).astype(jnp.bfloat16)
    ltab = np.stack(halves(np.stack(lmat))).astype(jnp.bfloat16)
    a3 = np.zeros((CX, B, 128))
    b3 = np.zeros((CX, WIN, 128))
    lx = np.zeros((CX, WIN, 128))
    for sub in range(CX):
        placed = np.zeros((B, WIN))
        placed[:, sub : sub + B] = sine
        hi, lo = halves(placed)
        a3[sub, :, :120] = np.concatenate([hi, hi, lo], axis=1)
        b3[sub, :, :96] = np.concatenate([hi.T, hi.T, lo.T], axis=1)
        lap_placed = np.zeros((WIN, WIN))
        lap_placed[sub : sub + B, sub : sub + B] = -0.5 * lap
        hi, lo = halves(lap_placed)
        lx[sub, :, :80] = np.concatenate([hi, lo], axis=1)
    return (
        ktab,
        ltab,
        inv,
        a3.astype(np.float32),
        b3.astype(np.float32),
        lx.astype(jnp.bfloat16),
    )


def fold_place(lane):
    y = lane // B
    z = lane % B
    hy = (y >= B // 2).astype(jnp.int32)
    hz = (z >= B // 2).astype(jnp.int32)
    yy = jnp.where(hy == 1, B - 1 - y, y)
    zz = jnp.where(hz == 1, B - 1 - z, z)
    return (hy * 2 + hz) * QUAD + yy * (B // 2) + zz


def butterfly(v):
    q = [v[:, i * QUAD : (i + 1) * QUAD] for i in range(4)]
    sy0, sy1, dy0, dy1 = q[0] + q[2], q[1] + q[3], q[0] - q[2], q[1] - q[3]
    return jnp.concatenate([sy0 + sy1, sy0 - sy1, dy0 + dy1, dy0 - dy1], axis=1)


def split(v):
    hi = v.astype(jnp.bfloat16)
    lo = (v - hi.astype(jnp.float32)).astype(jnp.bfloat16)
    return hi, lo


NT = (((1,), (1,)), ((), ()))
NN = (((1,), (0,)), ((), ()))


def dot3(v, hi_mat, lo_mat, dims):
    hi, lo = split(v)
    f = functools.partial(
        lax.dot_general, dimension_numbers=dims, preferred_element_type=jnp.float32
    )
    return f(hi, hi_mat) + f(lo, hi_mat) + f(hi, lo_mat)


def solve_kernel(
    idx_ref, shift_ref, partner_ref, member_ref,
    own_ref, mine_ref, sib_ref, pot_ref,
    ktab_ref, ltab_ref, inv_ref, a3_ref, b3_ref, lx_ref,
    out_ref,
    wv, acc, stg, pt, home, lm, lci, lcj, lsub, llo,
):
    slab = idx_ref[0]
    core = idx_ref[1]

    def widen(ci, _):
        c_mine = core * HALF + ci
        c_sib = (1 - core) * HALF + ci
        wv[c_mine, 0:CX] = own_ref[c_mine].astype(jnp.float32)
        wv[c_sib, 0:CX] = own_ref[c_sib].astype(jnp.float32)
        for k in range(WIDTH):
            rows = slice((k + 1) * CX, (k + 2) * CX)
            wv[c_mine, rows] = mine_ref[k, ci].astype(jnp.float32)
            wv[c_sib, rows] = sib_ref[k, ci].astype(jnp.float32)
        return 0

    lax.fori_loop(0, HALF, widen, 0)

    def find_home(c, count):
        home[count] = c
        return count + jnp.where(shift_ref[c] // CX == slab % WIDTH, 1, 0)

    lax.fori_loop(0, NCOL, find_home, jnp.int32(0))

    def list_slot(n, count):
        t = n // 56
        pid = partner_ref[n]
        a = t * MEMBERS + member_ref[n]
        live = jnp.logical_and(pid >= 0, a % 2 == core)
        pid = jnp.maximum(pid, 0)
        ci = home[a]
        cj = pid // 16
        rel = ((pid % 16) * B + shift_ref[cj] - slab * CX + 256) & 511
        lm[count] = a // 2
        lci[count] = ci
        lcj[count] = cj
        lsub[count] = shift_ref[ci] % CX
        llo[count] = rel - 256
        return count + jnp.where(live, 1, 0)

    count = lax.fori_loop(0, SLOTS, list_slot, jnp.int32(0))
    for extra in range(BATCH):
        lm[count + extra] = 0
        lci[count + extra] = 0
        lcj[count + extra] = 0
        lsub[count + extra] = 0
        llo[count + extra] = 1000

    row_ids = lax.broadcasted_iota(jnp.int32, (WIN, 1), 0)

    for group in range(2):
        for j in range(6):
            i = group * 6 + j
            c = home[2 * i + core]
            sub = shift_ref[c] % CX
            inside = jnp.logical_and(row_ids >= sub, row_ids < sub + B)
            w = jnp.where(inside, wv[c], 0.0)
            stg[j * WIN : (j + 1) * WIN] = butterfly(w)
            twice = jnp.concatenate([w, w], axis=0).astype(jnp.bfloat16)
            acc[i] = pot_ref[...] * w + jnp.dot(
                lx_ref[sub][:, :80], twice, preferred_element_type=jnp.float32
            )
        for q in range(4):
            cols = slice(q * QUAD, (q + 1) * QUAD)
            v = stg[0 : 6 * WIN, cols]
            stg[0 : 6 * WIN, cols] = dot3(v, ltab_ref[0, q], ltab_ref[1, q], NN)
        for j in range(6):
            i = group * 6 + j
            acc[i] = acc[i] + butterfly(stg[j * WIN : (j + 1) * WIN])

    lane_ids = lax.broadcasted_iota(jnp.int32, (1, 128), 1)
    lane_row = lane_ids - WIN * jnp.where(lane_ids >= WIN, 1, 0)
    lane_row = lane_row - WIN * jnp.where(lane_ids >= 2 * WIN, 1, 0)

    def batch(b, _):
        for p in range(BATCH):
            n = b * BATCH + p
            lo = llo[n]
            held = jnp.logical_and(lane_row >= lo, lane_row < lo + B)
            left = jnp.where(held, a3_ref[lsub[n]], 0.0).astype(jnp.bfloat16)
            dens = wv[lci[n]] * wv[lcj[n]]
            hi = dens.astype(jnp.bfloat16).astype(jnp.float32)
            stack = jnp.concatenate(
                [hi, dens - hi, hi, jnp.zeros((CX, CROSS), jnp.float32)], axis=0
            ).astype(jnp.bfloat16)
            u = jnp.dot(left, stack, preferred_element_type=jnp.float32)
            stg[p * B : (p + 1) * B] = butterfly(u)
        for q in range(4):
            cols = slice(q * QUAD, (q + 1) * QUAD)
            g = dot3(stg[:, cols], ktab_ref[0, q], ktab_ref[1, q], NN)
            g = g.reshape(BATCH, B, QUAD) * inv_ref[:, cols][None]
            g = g.reshape(BATCH * B, QUAD)
            stg[:, cols] = dot3(g, ktab_ref[0, q], ktab_ref[1, q], NT)
        for p in range(BATCH):
            n = b * BATCH + p
            lo = llo[n]
            held = jnp.logical_and(row_ids >= lo, row_ids < lo + B)
            right = jnp.where(held, b3_ref[lsub[n]], 0.0).astype(jnp.bfloat16)
            hi, low = split(butterfly(stg[p * B : (p + 1) * B]))
            stack = jnp.concatenate([hi, low, hi], axis=0)
            field = jnp.dot(right[:, :96], stack, preferred_element_type=jnp.float32)
            m = lm[n]
            acc[m] = acc[m] + field * wv[lcj[n]]
        return 0

    lax.fori_loop(0, (count + BATCH - 1) // BATCH, batch, 0)

    for q in range(4):
        place = fold_place(lax.broadcasted_iota(jnp.int32, (1, QUAD), 1) + q * QUAD)
        rows = lax.broadcasted_iota(jnp.int32, (CROSS, QUAD), 0)
        pt[:, q * QUAD : (q + 1) * QUAD] = jnp.where(rows == place, 1.0, 0.0).astype(
            jnp.bfloat16
        )
    for group in range(2):
        v = acc[group * 6 : group * 6 + 6].reshape(6 * WIN, CROSS)
        hi, lo = split(v)
        for q in range(4):
            cols = slice(q * QUAD, (q + 1) * QUAD)
            y = jnp.dot(hi, pt[:, cols], preferred_element_type=jnp.float32) + jnp.dot(
                lo, pt[:, cols], preferred_element_type=jnp.float32
            )
            for j in range(6):
                for k in range(WIDTH + 1):
                    first = j * WIN + k * CX
                    out_ref[k, group * 6 + j, :, cols] = y[first : first + CX]


def place_kernel(idx_ref, shift_ref, mine_ref, sib_ref, out_ref, rank):
    slab = idx_ref[0]
    core = idx_ref[1]
    for cl in range(WIDTH):
        rank[cl] = 0

    def one(c, _):
        cl = shift_ref[c] // CX
        a = rank[cl]
        rank[cl] = a + 1
        k = (slab - cl) & 3
        i = a // 2
        from_mine = a % 2 == core

        @pl.when(jnp.logical_and(from_mine, k > 0))
        def _():
            out_ref[c] = mine_ref[k, i]

        @pl.when(jnp.logical_and(from_mine, k == 0))
        def _():
            out_ref[c] = mine_ref[0, i] + mine_ref[WIDTH, i]

        @pl.when(jnp.logical_and(jnp.logical_not(from_mine), k > 0))
        def _():
            out_ref[c] = sib_ref[k, i]

        @pl.when(jnp.logical_and(jnp.logical_not(from_mine), k == 0))
        def _():
            out_ref[c] = sib_ref[0, i] + sib_ref[WIDTH, i]

        return 0

    lax.fori_loop(0, NCOL, one, 0)


def forward_route(step):
    pairs = []
    for group in range(4):
        zh, core = group // 2, group % 2
        for s in range(SLABS):
            to = (s + step) % SLABS
            turn = 1 if (s // 4) % 4 == 3 and (to // 4) % 4 == 0 else 0
            there = (zh ^ turn) * 2 + core
            pairs.append((group * SLABS + s, there * SLABS + to))
    return pairs


def ahead(x, step):
    return lax.ppermute(x, ("group", "orb"), forward_route(step))


def behind(x, step):
    return lax.ppermute(x, ("group", "orb"), [(j, i) for i, j in forward_route(step)])


def swap_cores(x):
    return lax.ppermute(x, "group", [(0, 1), (1, 0), (2, 3), (3, 2)])


def body(orbitals, potential, box_shift, pair_partner, pair_member):
    ktab, ltab, inv, a3, b3, lx = tables()
    slab = lax.axis_index("orb").astype(jnp.int32)
    core = lax.axis_index("group").astype(jnp.int32) % 2
    lanes = jnp.arange(CROSS, dtype=jnp.int32)
    fold = (fold_place(lanes)[:, None] == lanes[None, :]).astype(jnp.bfloat16)
    own = jnp.dot(
        orbitals.reshape(NCOL * CX, CROSS), fold, preferred_element_type=jnp.bfloat16
    ).reshape(NCOL, CX, CROSS)
    pot = jnp.dot(
        potential, fold.astype(jnp.float32), precision=lax.Precision.HIGHEST
    )
    half = lax.dynamic_slice_in_dim(own, core * HALF, HALF, 0)
    mine = jnp.stack([behind(half, k) for k in range(1, WIDTH + 1)])
    pots = jnp.concatenate([pot] + [behind(pot, k) for k in range(1, WIDTH + 1)], axis=0)
    sib = swap_cores(mine)
    idx = jnp.stack([slab, core])
    partners = lax.dynamic_slice_in_dim(pair_partner, slab * 3, 3, 0).reshape(-1)
    members = lax.dynamic_slice_in_dim(pair_member, slab * 3, 3, 0).reshape(-1)
    smem = pl.BlockSpec(memory_space=pltpu.SMEM)
    vmem = pl.BlockSpec(memory_space=pltpu.VMEM)
    boxes = pl.pallas_call(
        solve_kernel,
        out_shape=jax.ShapeDtypeStruct((WIDTH + 1, MINE, CX, CROSS), jnp.float32),
        in_specs=[smem] * 4 + [vmem] * 10,
        out_specs=vmem,
        scratch_shapes=[
            pltpu.VMEM((NCOL, WIN, CROSS), jnp.float32),
            pltpu.VMEM((MINE, WIN, CROSS), jnp.float32),
            pltpu.VMEM((BATCH * B, CROSS), jnp.float32),
            pltpu.VMEM((CROSS, CROSS), jnp.bfloat16),
            pltpu.SMEM((32,), jnp.int32),
        ]
        + [pltpu.SMEM((SLOTS + BATCH,), jnp.int32)] * 5,
        compiler_params=pltpu.CompilerParams(vmem_limit_bytes=60 * 2**20),
        name="solve",
    )(idx, box_shift, partners, members, own, mine, sib, pots, ktab, ltab, inv, a3, b3, lx)
    got = jnp.stack([boxes[0]] + [ahead(boxes[k], k) for k in range(1, WIDTH + 1)])
    other = swap_cores(got)
    return pl.pallas_call(
        place_kernel,
        out_shape=jax.ShapeDtypeStruct((NCOL, CX, CROSS), jnp.float32),
        in_specs=[smem] * 2 + [vmem] * 2,
        out_specs=vmem,
        scratch_shapes=[pltpu.SMEM((WIDTH,), jnp.int32)],
        compiler_params=pltpu.CompilerParams(vmem_limit_bytes=40 * 2**20),
        name="place",
    )(idx, box_shift, got, other)


def solution(mesh):
    placed = (P(None, "orb", None), P("orb", None), P(), P(), P())
    return jax.shard_map(
        body, mesh=mesh, in_specs=placed, out_specs=P(None, "orb", None), check_vma=False
    )
```

profile of v0, /device:TPU:19, one launch (start us, length us, event | category | flops | bytes accessed | tf_op | source)
XLA Modules:
  0.0 181.9 jit_solution(6947960804959421434)
XLA Ops:
  0.0 0.0 copy-start
  0.0 1.4 copy-done
  1.4 2.1 %fusion.5.own_ref = bf16[96,8,1024]{2,1,0:T(8,128)(2,1)S(1)} fusion(bf16[96,8,1024]{2,1,0:T(8,128)(2,1)S(1)} %copy-done, s32[1024]{0:T(1024)S(1)} %fusion.17), kind=kOutput, calls=%fused_computation.7 | convolution fusion | flops 1611661312 | bytes 3149824 | tf_op jit(solution)/shard_map/dot_general | solution.py:319
  3.5 0.0 copy-start.3
  3.5 0.1 constant_dynamic-slice_fusion
  3.6 5.6 %collective-permute-start.3 = (bf16[48,8,1024]{2,1,0:T(8,128)(2,1)S(1)}, bf16[48,8,1024]{2,1,0:T(8,128)(2,1)S(1)}, u32[]{:S(2)}, u32[]{:S(2)}) collective-permute-start(bf16[48,8,1024]{2,1,0:T(8,128)(2,1)S(1)} %constant_dynamic-slice_fusion), channel_id=1, source_target_pairs={{4,0},{5,1},{6,2},{7,3},{8,4},{9,5},{10,6},{11,7},{12,8},{13,9},{1... | collective-permute-start | bytes 2359304 | tf_op jit(solution)/shard_map/ppermute | solution.py:306
  9.2 1.4 collective-permute-start.2
  10.6 0.4 collective-permute-start.1
  11.0 0.8 collective-permute-start
  11.8 13.6 %collective-permute-done.3 = bf16[48,8,1024]{2,1,0:T(8,128)(2,1)S(1)} collective-permute-done((bf16[48,8,1024]{2,1,0:T(8,128)(2,1)S(1)}, bf16[48,8,1024]{2,1,0:T(8,128)(2,1)S(1)}, u32[]{:S(2)}, u32[]{:S(2)}) %collective-permute-start.3) | collective-permute-done | bytes 786464 | tf_op jit(solution)/shard_map/ppermute | solution.py:306
  25.4 16.9 %collective-permute-done.2 = bf16[48,8,1024]{2,1,0:T(8,128)(2,1)S(1)} collective-permute-done((bf16[48,8,1024]{2,1,0:T(8,128)(2,1)S(1)}, bf16[48,8,1024]{2,1,0:T(8,128)(2,1)S(1)}, u32[]{:S(2)}, u32[]{:S(2)}) %collective-permute-start.2) | collective-permute-done | bytes 786464 | tf_op jit(solution)/shard_map/ppermute | solution.py:306
  42.3 13.6 %collective-permute-done.1 = bf16[48,8,1024]{2,1,0:T(8,128)(2,1)S(1)} collective-permute-done((bf16[48,8,1024]{2,1,0:T(8,128)(2,1)S(1)}, bf16[48,8,1024]{2,1,0:T(8,128)(2,1)S(1)}, u32[]{:S(2)}, u32[]{:S(2)}) %collective-permute-start.1) | collective-permute-done | bytes 786464 | tf_op jit(solution)/shard_map/ppermute | solution.py:306
  55.9 0.0 collective-permute-done
  55.9 0.0 copy-start.7
  55.9 0.0 copy-start.5
  55.9 0.0 copy-start.6
  55.9 1.9 %pad_maximum_fusion.mine_ref = bf16[4,48,8,1024]{3,2,1,0:T(8,128)(2,1)} fusion(bf16[1,48,8,1024]{3,2,1,0:T(8,128)(2,1)S(1)} %bitcast.34, bf16[1,48,8,1024]{3,2,1,0:T(8,128)(2,1)S(1)} %bitcast.35, bf16[1,48,8,1024]{3,2,1,0:T(8,128)(2,1)S(1)} %bitcast.36, bf16[1,48,8,1024]{3,2,1,0:T(8,128)(2,1)S(1)} %bitcast.37), kind=kLoop, calls=%fused_computation.3 | loop fusion | flops 4718592 | bytes 6291456 | tf_op jit(solution)/shard_map/stack | solution.py:326
  57.8 0.0 copy-done.3
  57.8 2.3 %collective-permute-start.4 = (bf16[4,48,8,1024]{3,2,1,0:T(8,128)(2,1)}, bf16[4,48,8,1024]{3,2,1,0:T(8,128)(2,1)}, u32[]{:S(2)}, u32[]{:S(2)}) collective-permute-start(bf16[4,48,8,1024]{3,2,1,0:T(8,128)(2,1)} %pad_maximum_fusion.mine_ref), channel_id=1, source_target_pairs={{0,64},{64,0},{128,192},{192,128},{1,65},{65,1},{129,193},{193,129... | collective-permute-start | bytes 9437192 | tf_op jit(solution)/shard_map/ppermute | solution.py:310
  60.1 0.0 copy-done.7
  60.1 1.5 constant_dynamic-update-slice_fusion.4
  61.6 7.7 %collective-permute-start.8 = (f32[8,1024]{1,0:T(8,128)S(1)}, f32[8,1024]{1,0:T(8,128)S(1)}, u32[]{:S(2)}, u32[]{:S(2)}) collective-permute-start(f32[8,1024]{1,0:T(8,128)S(1)} %get-tuple-element.11), channel_id=1, source_target_pairs={{4,0},{5,1},{6,2},{7,3},{8,4},{9,5},{10,6},{11,7},{12,8},{13,9},{1... | collective-permute-start | bytes 98312 | tf_op jit(solution)/shard_map/ppermute | solution.py:306
  69.2 17.4 %collective-permute-start.7 = (f32[8,1024]{1,0:T(8,128)S(1)}, f32[8,1024]{1,0:T(8,128)S(1)}, u32[]{:S(2)}, u32[]{:S(2)}) collective-permute-start(f32[8,1024]{1,0:T(8,128)S(1)} %get-tuple-element.11), channel_id=1, source_target_pairs={{3,0},{4,1},{5,2},{6,3},{7,4},{8,5},{9,6},{10,7},{11,8},{12,9},{13... | collective-permute-start | bytes 98312 | tf_op jit(solution)/shard_map/ppermute | solution.py:306
  86.6 0.0 collective-permute-start.6
  86.7 1.3 collective-permute-start.5
  87.9 0.0 copy-done.5
  87.9 0.0 copy-done.6
  87.9 0.1 constant_dynamic-slice_fusion.1
  88.0 0.7 pad_add_fusion.idx_ref
  88.7 0.1 copy.13
  88.7 0.7 reshape.49.member_ref
  89.4 0.1 copy.12
  89.5 0.7 reshape.48.partner_ref
  90.2 0.0 collective-permute-done.5
  90.2 1.7 collective-permute-done.6
  91.8 0.0 collective-permute-done.7
  91.8 0.0 collective-permute-done.8
  91.9 0.0 copy-start.4
  91.9 0.0 collective-permute-done.4.sib_ref
  91.9 0.7 copy-done.4
  92.5 24.5 %solve.1 = f32[5,12,8,1024]{3,2,1,0:T(8,128)} custom-call(s32[2]{0:T(128)} %pad_add_fusion.idx_ref, s32[96]{0:T(128)} %shift_ref.3, s32[168]{0:T(256)} %reshape.48.partner_ref, s32[168]{0:T(256)} %reshape.49.member_ref, bf16[96,8,1024]{2,1,0:T(8,128)(2,1)} %copy-done.3, bf16[4,48,8,1024]{3,2,1,0:T(8,128)(2,1)} %pad_maximum_fusion.mine_ref, ...), custom_call_target="tpu_custom_call" | custom-call | tf_op jit(solution)/shard_map/solve/pallas_call | solution.py:334
  117.0 1.7 slice_bitcast_fusion
  118.7 0.0 copy-start.1
  118.7 0.0 copy-start.2
  118.7 0.1 collective-permute-start.9
  118.8 1.6 collective-permute-start.10
  120.4 4.2 %collective-permute-start.12 = (f32[12,8,1024]{2,1,0:T(8,128)S(1)}, f32[12,8,1024]{2,1,0:T(8,128)S(1)}, u32[]{:S(2)}, u32[]{:S(2)}) collective-permute-start(f32[12,8,1024]{2,1,0:T(8,128)S(1)} %get-tuple-element.5), channel_id=1, source_target_pairs={{0,4},{1,5},{2,6},{3,7},{4,8},{5,9},{6,10},{7,11},{8,12},{9,13},{1... | collective-permute-start | bytes 1179656 | tf_op jit(solution)/shard_map/ppermute | solution.py:302
  124.6 0.0 collective-permute-start.11
  124.6 3.5 %collective-permute-done.9 = f32[12,8,1024]{2,1,0:T(8,128)S(1)} collective-permute-done((f32[12,8,1024]{2,1,0:T(8,128)S(1)}, f32[12,8,1024]{2,1,0:T(8,128)S(1)}, u32[]{:S(2)}, u32[]{:S(2)}) %collective-permute-start.9) | collective-permute-done | bytes 393248 | tf_op jit(solution)/shard_map/ppermute | solution.py:302
  128.1 14.5 %collective-permute-done.10 = f32[12,8,1024]{2,1,0:T(8,128)S(1)} collective-permute-done((f32[12,8,1024]{2,1,0:T(8,128)S(1)}, f32[12,8,1024]{2,1,0:T(8,128)S(1)}, u32[]{:S(2)}, u32[]{:S(2)}) %collective-permute-start.10) | collective-permute-done | bytes 393248 | tf_op jit(solution)/shard_map/ppermute | solution.py:302
  142.6 28.1 %collective-permute-done.11 = f32[12,8,1024]{2,1,0:T(8,128)S(1)} collective-permute-done((f32[12,8,1024]{2,1,0:T(8,128)S(1)}, f32[12,8,1024]{2,1,0:T(8,128)S(1)}, u32[]{:S(2)}, u32[]{:S(2)}) %collective-permute-start.11) | collective-permute-done | bytes 393248 | tf_op jit(solution)/shard_map/ppermute | solution.py:302
  170.7 0.0 collective-permute-done.12
  170.7 0.7 collective-permute-start.13
  171.4 3.6 %collective-permute-done.13.sib_ref = f32[5,12,8,1024]{3,2,1,0:T(8,128)S(1)} collective-permute-done((f32[5,12,8,1024]{3,2,1,0:T(8,128)S(1)}, f32[5,12,8,1024]{3,2,1,0:T(8,128)S(1)}, u32[]{:S(2)}, u32[]{:S(2)}) %collective-permute-start.13) | collective-permute-done | bytes 1966112 | tf_op jit(solution)/shard_map/ppermute | solution.py:310
  175.0 0.0 copy-done.1
  175.0 0.0 copy-done.2
  175.0 6.8 %place.1 = f32[96,8,1024]{2,1,0:T(8,128)} custom-call(s32[2]{0:T(128)S(1)} %copy-done.2, s32[96]{0:T(128)S(1)} %copy-done.1, f32[5,12,8,1024]{3,2,1,0:T(8,128)S(1)} %bitcast_dynamic-update-slice_fusion.mine_ref, f32[5,12,8,1024]{3,2,1,0:T(8,128)S(1)} %collective-permute-done.13.sib_ref), custom_call_target="tpu_custom_call" | custom-call | tf_op jit(solution)/shard_map/place/pallas_call | solution.py:352
  (9 shorter events, 0.1 us)
Async XLA Ops:
  0.0 1.4 copy-start
  3.5 54.3 %copy-start.3 = (bf16[96,8,1024]{2,1,0:T(8,128)(2,1)}, bf16[96,8,1024]{2,1,0:T(8,128)(2,1)S(1)}, u32[]{:S(2)}) copy-start(bf16[96,8,1024]{2,1,0:T(8,128)(2,1)S(1)} %fusion.5.own_ref) | copy-start | bytes 4718596
  3.6 21.9 %collective-permute-start.3 = (bf16[48,8,1024]{2,1,0:T(8,128)(2,1)S(1)}, bf16[48,8,1024]{2,1,0:T(8,128)(2,1)S(1)}, u32[]{:S(2)}, u32[]{:S(2)}) collective-permute-start(bf16[48,8,1024]{2,1,0:T(8,128)(2,1)S(1)} %constant_dynamic-slice_fusion), channel_id=1, source_target_pairs={{4,0},{5,1},{6,2},{7,3},{8,4},{9,5},{10,6},{11,7},{12,8},{13,9},{1... | collective-permute-start | bytes 2359304 | tf_op jit(solution)/shard_map/ppermute | solution.py:306
  9.2 33.1 %collective-permute-start.2 = (bf16[48,8,1024]{2,1,0:T(8,128)(2,1)S(1)}, bf16[48,8,1024]{2,1,0:T(8,128)(2,1)S(1)}, u32[]{:S(2)}, u32[]{:S(2)}) collective-permute-start(bf16[48,8,1024]{2,1,0:T(8,128)(2,1)S(1)} %constant_dynamic-slice_fusion), channel_id=1, source_target_pairs={{3,0},{4,1},{5,2},{6,3},{7,4},{8,5},{9,6},{10,7},{11,8},{12,9},{13... | collective-permute-start | bytes 2359304 | tf_op jit(solution)/shard_map/ppermute | solution.py:306
  10.6 45.3 %collective-permute-start.1 = (bf16[48,8,1024]{2,1,0:T(8,128)(2,1)S(1)}, bf16[48,8,1024]{2,1,0:T(8,128)(2,1)S(1)}, u32[]{:S(2)}, u32[]{:S(2)}) collective-permute-start(bf16[48,8,1024]{2,1,0:T(8,128)(2,1)S(1)} %constant_dynamic-slice_fusion), channel_id=1, source_target_pairs={{2,0},{3,1},{4,2},{5,3},{6,4},{7,5},{8,6},{9,7},{10,8},{11,9},{12,... | collective-permute-start | bytes 2359304 | tf_op jit(solution)/shard_map/ppermute | solution.py:306
  11.0 44.9 %collective-permute-start = (bf16[48,8,1024]{2,1,0:T(8,128)(2,1)S(1)}, bf16[48,8,1024]{2,1,0:T(8,128)(2,1)S(1)}, u32[]{:S(2)}, u32[]{:S(2)}) collective-permute-start(bf16[48,8,1024]{2,1,0:T(8,128)(2,1)S(1)} %constant_dynamic-slice_fusion), channel_id=1, source_target_pairs={{1,0},{2,1},{3,2},{4,3},{5,4},{6,5},{7,6},{8,7},{9,8},{10,9},{11,1... | collective-permute-start | bytes 2359304 | tf_op jit(solution)/shard_map/ppermute | solution.py:306
  55.9 4.2 %copy-start.7 = (f32[8,1024]{1,0:T(8,128)S(1)}, f32[8,1024]{1,0:T(8,128)}, u32[]{:S(2)}) copy-start(f32[8,1024]{1,0:T(8,128)} %param.12) | copy-start | bytes 98308
  55.9 32.0 %copy-start.5 = (s32[192,56]{0,1:T(8,128)S(1)}, s32[192,56]{0,1:T(8,128)}, u32[]{:S(2)}) copy-start(s32[192,56]{0,1:T(8,128)} %param.15) | copy-start | bytes 129028
  55.9 32.0 %copy-start.6 = (s32[192,56]{0,1:T(8,128)S(1)}, s32[192,56]{0,1:T(8,128)}, u32[]{:S(2)}) copy-start(s32[192,56]{0,1:T(8,128)} %param.14) | copy-start | bytes 129028
  57.8 34.1 %collective-permute-start.4 = (bf16[4,48,8,1024]{3,2,1,0:T(8,128)(2,1)}, bf16[4,48,8,1024]{3,2,1,0:T(8,128)(2,1)}, u32[]{:S(2)}, u32[]{:S(2)}) collective-permute-start(bf16[4,48,8,1024]{3,2,1,0:T(8,128)(2,1)} %pad_maximum_fusion.mine_ref), channel_id=1, source_target_pairs={{0,64},{64,0},{128,192},{192,128},{1,65},{65,1},{129,193},{193,129... | collective-permute-start | bytes 9437192 | tf_op jit(solution)/shard_map/ppermute | solution.py:310
  61.6 30.3 %collective-permute-start.8 = (f32[8,1024]{1,0:T(8,128)S(1)}, f32[8,1024]{1,0:T(8,128)S(1)}, u32[]{:S(2)}, u32[]{:S(2)}) collective-permute-start(f32[8,1024]{1,0:T(8,128)S(1)} %get-tuple-element.11), channel_id=1, source_target_pairs={{4,0},{5,1},{6,2},{7,3},{8,4},{9,5},{10,6},{11,7},{12,8},{13,9},{1... | collective-permute-start | bytes 98312 | tf_op jit(solution)/shard_map/ppermute | solution.py:306
  69.2 22.6 %collective-permute-start.7 = (f32[8,1024]{1,0:T(8,128)S(1)}, f32[8,1024]{1,0:T(8,128)S(1)}, u32[]{:S(2)}, u32[]{:S(2)}) collective-permute-start(f32[8,1024]{1,0:T(8,128)S(1)} %get-tuple-element.11), channel_id=1, source_target_pairs={{3,0},{4,1},{5,2},{6,3},{7,4},{8,5},{9,6},{10,7},{11,8},{12,9},{13... | collective-permute-start | bytes 98312 | tf_op jit(solution)/shard_map/ppermute | solution.py:306
  86.6 5.2 %collective-permute-start.6 = (f32[8,1024]{1,0:T(8,128)S(1)}, f32[8,1024]{1,0:T(8,128)S(1)}, u32[]{:S(2)}, u32[]{:S(2)}) collective-permute-start(f32[8,1024]{1,0:T(8,128)S(1)} %get-tuple-element.11), channel_id=1, source_target_pairs={{2,0},{3,1},{4,2},{5,3},{6,4},{7,5},{8,6},{9,7},{10,8},{11,9},{12,... | collective-permute-start | bytes 98312 | tf_op jit(solution)/shard_map/ppermute | solution.py:306
  86.7 3.5 %collective-permute-start.5 = (f32[8,1024]{1,0:T(8,128)S(1)}, f32[8,1024]{1,0:T(8,128)S(1)}, u32[]{:S(2)}, u32[]{:S(2)}) collective-permute-start(f32[8,1024]{1,0:T(8,128)S(1)} %get-tuple-element.11), channel_id=1, source_target_pairs={{1,0},{2,1},{3,2},{4,3},{5,4},{6,5},{7,6},{8,7},{9,8},{10,9},{11,1... | collective-permute-start | bytes 98312 | tf_op jit(solution)/shard_map/ppermute | solution.py:306
  91.9 0.7 copy-start.4
  118.7 56.3 %copy-start.1 = (s32[96]{0:T(128)S(1)}, s32[96]{0:T(128)}, u32[]{:S(2)}) copy-start(s32[96]{0:T(128)} %shift_ref.3) | copy-start | bytes 1156
  118.7 56.3 %copy-start.2 = (s32[2]{0:T(128)S(1)}, s32[2]{0:T(128)}, u32[]{:S(2)}) copy-start(s32[2]{0:T(128)} %pad_add_fusion.idx_ref) | copy-start | bytes 28
  118.7 9.3 %collective-permute-start.9 = (f32[12,8,1024]{2,1,0:T(8,128)S(1)}, f32[12,8,1024]{2,1,0:T(8,128)S(1)}, u32[]{:S(2)}, u32[]{:S(2)}) collective-permute-start(f32[12,8,1024]{2,1,0:T(8,128)S(1)} %get-tuple-element.8), channel_id=1, source_target_pairs={{0,1},{1,2},{2,3},{3,4},{4,5},{5,6},{6,7},{7,8},{8,9},{9,10},{10,1... | collective-permute-start | bytes 1179656 | tf_op jit(solution)/shard_map/ppermute | solution.py:302
  118.8 23.7 %collective-permute-start.10 = (f32[12,8,1024]{2,1,0:T(8,128)S(1)}, f32[12,8,1024]{2,1,0:T(8,128)S(1)}, u32[]{:S(2)}, u32[]{:S(2)}) collective-permute-start(f32[12,8,1024]{2,1,0:T(8,128)S(1)} %get-tuple-element.7), channel_id=1, source_target_pairs={{0,2},{1,3},{2,4},{3,5},{4,6},{5,7},{6,8},{7,9},{8,10},{9,11},{10,... | collective-permute-start | bytes 1179656 | tf_op jit(solution)/shard_map/ppermute | solution.py:302
  120.4 50.3 %collective-permute-start.12 = (f32[12,8,1024]{2,1,0:T(8,128)S(1)}, f32[12,8,1024]{2,1,0:T(8,128)S(1)}, u32[]{:S(2)}, u32[]{:S(2)}) collective-permute-start(f32[12,8,1024]{2,1,0:T(8,128)S(1)} %get-tuple-element.5), channel_id=1, source_target_pairs={{0,4},{1,5},{2,6},{3,7},{4,8},{5,9},{6,10},{7,11},{8,12},{9,13},{1... | collective-permute-start | bytes 1179656 | tf_op jit(solution)/shard_map/ppermute | solution.py:302
  124.6 46.1 %collective-permute-start.11 = (f32[12,8,1024]{2,1,0:T(8,128)S(1)}, f32[12,8,1024]{2,1,0:T(8,128)S(1)}, u32[]{:S(2)}, u32[]{:S(2)}) collective-permute-start(f32[12,8,1024]{2,1,0:T(8,128)S(1)} %get-tuple-element.6), channel_id=1, source_target_pairs={{0,3},{1,4},{2,5},{3,6},{4,7},{5,8},{6,9},{7,10},{8,11},{9,12},{10... | collective-permute-start | bytes 1179656 | tf_op jit(solution)/shard_map/ppermute | solution.py:302
  170.7 4.3 %collective-permute-start.13 = (f32[5,12,8,1024]{3,2,1,0:T(8,128)S(1)}, f32[5,12,8,1024]{3,2,1,0:T(8,128)S(1)}, u32[]{:S(2)}, u32[]{:S(2)}) collective-permute-start(f32[5,12,8,1024]{3,2,1,0:T(8,128)S(1)} %bitcast_dynamic-update-slice_fusion.mine_ref), channel_id=1, source_target_pairs={{0,64},{64,0},{128,192},{192,128},{1,65},{65,1},{129,193},{193,129... | collective-permute-start | bytes 5898248 | tf_op jit(solution)/shard_map/ppermute | solution.py:310
where the time goes:
time: 182 us
  waiting for transfers between devices  95.4 us (52%)
  starting transfers between devices  43.5 us (24%)
  Pallas kernels  31.3 us (17%)
  local copies, waits for them, and re-layouts  5.5 us (3%)
  matrix products  3.52 us (2%)
  other arithmetic  2.55 us (1%)
    ppermute x4, waiting for transfers between devices, ahead(): return lax.ppermute(x, ('group', 'orb'), forward_route(step))  46 us
    ppermute x8, waiting for transfers between devices, behind(): lax.ppermute(x, ('group', 'orb'), [(j, i) for i, j in forward_route(step)])  45.7 us
    ppermute x8, starting transfers between devices, behind(): lax.ppermute(x, ('group', 'orb'), [(j, i) for i, j in forward_route(step)])  34.6 us
    pallas_call x1, Pallas kernels, body(): pl.pallas_call(solve_kernel, out_shape=jax.ShapeDtypeStruct((WIDTH + 1, M...  24.5 us
    pallas_call x1, Pallas kernels, body(): pl.pallas_call(place_kernel, out_shape=jax.ShapeDtypeStruct((NCOL, CX, CR...  6.82 us
    ppermute x4, starting transfers between devices, ahead(): return lax.ppermute(x, ('group', 'orb'), forward_route(step))  5.84 us
  transfers between devices with their start and end apart: 14, of which 8 were waited for; matrix products, arithmetic and copies ran while one was open for 2% of the time, Pallas kernels for 0%

commit v1 on v0

--- a/solution.py
+++ b/solution.py
@@ -21,6 +21,10 @@
 MINE = 12
 BATCH = 8
 SLOTS = 168
+PIECES = 4
+PIECE = HALF // PIECES
+SHIPS = 2
+BOXES = MINE // SHIPS
 
 lap_weights = (
     -5369.0 / 1800.0,
@@ -121,7 +125,7 @@
 
 def solve_kernel(
     idx_ref, shift_ref, partner_ref, member_ref,
-    own_ref, mine_ref, sib_ref, pot_ref,
+    own_ref, win_ref, pot_ref, potw_ref,
     ktab_ref, ltab_ref, inv_ref, a3_ref, b3_ref, lx_ref,
     out_ref,
     wv, acc, stg, pt, home, lm, lci, lcj, lsub, llo,
@@ -129,18 +133,14 @@
     slab = idx_ref[0]
     core = idx_ref[1]
 
-    def widen(ci, _):
-        c_mine = core * HALF + ci
-        c_sib = (1 - core) * HALF + ci
-        wv[c_mine, 0:CX] = own_ref[c_mine].astype(jnp.float32)
-        wv[c_sib, 0:CX] = own_ref[c_sib].astype(jnp.float32)
+    def widen(c, _):
+        wv[c, 0:CX] = own_ref[c].astype(jnp.float32)
         for k in range(WIDTH):
-            rows = slice((k + 1) * CX, (k + 2) * CX)
-            wv[c_mine, rows] = mine_ref[k, ci].astype(jnp.float32)
-            wv[c_sib, rows] = sib_ref[k, ci].astype(jnp.float32)
+            wv[c, (k + 1) * CX : (k + 2) * CX] = win_ref[k, c].astype(jnp.float32)
         return 0
 
-    lax.fori_loop(0, HALF, widen, 0)
+    lax.fori_loop(0, NCOL, widen, 0)
+    pots = jnp.concatenate([pot_ref[...], potw_ref[...].reshape(WIDTH * CX, CROSS)], axis=0)
 
     def find_home(c, count):
         home[count] = c
@@ -183,7 +183,7 @@
             w = jnp.where(inside, wv[c], 0.0)
             stg[j * WIN : (j + 1) * WIN] = butterfly(w)
             twice = jnp.concatenate([w, w], axis=0).astype(jnp.bfloat16)
-            acc[i] = pot_ref[...] * w + jnp.dot(
+            acc[i] = pots * w + jnp.dot(
                 lx_ref[sub][:, :80], twice, preferred_element_type=jnp.float32
             )
         for q in range(4):
@@ -251,7 +251,7 @@
                     out_ref[k, group * 6 + j, :, cols] = y[first : first + CX]
 
 
-def place_kernel(idx_ref, shift_ref, mine_ref, sib_ref, out_ref, rank):
+def place_kernel(idx_ref, shift_ref, mine_ref, sib_ref, got_ref, out_ref, rank):
     slab = idx_ref[0]
     core = idx_ref[1]
     for cl in range(WIDTH):
@@ -263,51 +263,170 @@
         rank[cl] = a + 1
         k = (slab - cl) & 3
         i = a // 2
-        from_mine = a % 2 == core
-
-        @pl.when(jnp.logical_and(from_mine, k > 0))
+        side = a % 2
+
+        @pl.when(k > 0)
         def _():
-            out_ref[c] = mine_ref[k, i]
-
-        @pl.when(jnp.logical_and(from_mine, k == 0))
+            out_ref[c] = got_ref[k - 1, side, i]
+
+        @pl.when(jnp.logical_and(k == 0, side == core))
         def _():
-            out_ref[c] = mine_ref[0, i] + mine_ref[WIDTH, i]
-
-        @pl.when(jnp.logical_and(jnp.logical_not(from_mine), k > 0))
+            out_ref[c] = got_ref[WIDTH - 1, side, i] + mine_ref[i]
+
+        @pl.when(jnp.logical_and(k == 0, side != core))
         def _():
-            out_ref[c] = sib_ref[k, i]
-
-        @pl.when(jnp.logical_and(jnp.logical_not(from_mine), k == 0))
-        def _():
-            out_ref[c] = sib_ref[0, i] + sib_ref[WIDTH, i]
+            out_ref[c] = got_ref[WIDTH - 1, side, i] + sib_ref[i]
 
         return 0
 
     lax.fori_loop(0, NCOL, one, 0)
 
 
-def forward_route(step):
-    pairs = []
-    for group in range(4):
-        zh, core = group // 2, group % 2
-        for s in range(SLABS):
-            to = (s + step) % SLABS
-            turn = 1 if (s // 4) % 4 == 3 and (to // 4) % 4 == 0 else 0
-            there = (zh ^ turn) * 2 + core
-            pairs.append((group * SLABS + s, there * SLABS + to))
-    return pairs
-
-
-def ahead(x, step):
-    return lax.ppermute(x, ("group", "orb"), forward_route(step))
-
-
-def behind(x, step):
-    return lax.ppermute(x, ("group", "orb"), [(j, i) for i, j in forward_route(step)])
-
-
-def swap_cores(x):
-    return lax.ppermute(x, "group", [(0, 1), (1, 0), (2, 3), (3, 2)])
+def slab_at(step):
+    s = lax.axis_index("orb")
+    group = lax.axis_index("group")
+    y, zl, zh, core = s % 4, (s // 4) % 4, group // 2, group % 2
+    if step > 0:
+        turn = (zl + (y + step) // 4) // 4
+    else:
+        turn = 1 - (zl - (1 - (y + step + 4) // 4) + 4) // 4
+    return ((zh + turn) % 2 * 2 + core, (s + step + SLABS) % SLABS)
+
+
+def sibling():
+    group = lax.axis_index("group")
+    return (group // 2 * 2 + 1 - group % 2, lax.axis_index("orb"))
+
+
+def greet():
+    barrier = pltpu.get_barrier_semaphore()
+    others = [slab_at(step) for step in (-4, -3, -2, -1, 1, 2, 3, 4)] + [sibling()]
+    for other in others:
+        pl.semaphore_signal(
+            barrier, inc=1, device_id=other, device_id_type=pl.DeviceIdType.MESH
+        )
+    pl.semaphore_wait(barrier, len(others))
+
+
+def remote(src, dst, send, recv, device):
+    return pltpu.make_async_remote_copy(
+        src_ref=src,
+        dst_ref=dst,
+        send_sem=send,
+        recv_sem=recv,
+        device_id=device,
+        device_id_type=pl.DeviceIdType.MESH,
+    )
+
+
+def fetch_kernel(own, pot, win, potw, send, recv, dsend, drecv, psend, precv):
+    core = lax.axis_index("group") % 2
+    y = lax.axis_index("orb") % 4
+    greet()
+
+    def part(q):
+        return pl.ds(core * HALF + q * PIECE, PIECE)
+
+    def held(k, q):
+        return win.at[k - 1, part(q)]
+
+    down, up = slab_at(-1), slab_at(1)
+    low, high = slab_at(-3), slab_at(3)
+
+    def move(stream, src, k, q, device):
+        return remote(src, held(k, q), send.at[stream, q], recv.at[k - 1, q], device)
+
+    def to_sibling(k, q):
+        return remote(
+            held(k, q), held(k, q), dsend.at[k - 1, q], drecv.at[k - 1, q], sibling()
+        )
+
+    def pot_copy(k):
+        return remote(pot, potw.at[k - 1], psend.at[k - 1], precv.at[k - 1], slab_at(-k))
+
+    copies = {
+        0: (None, lambda q: move(0, own.at[part(q)], 4, q, slab_at(-4))),
+        1: (y >= 1, lambda q: move(1, own.at[part(q)], 1, q, down)),
+        2: (y == 3, lambda q: move(2, own.at[part(q)], 3, q, low)),
+        3: (y <= 2, lambda q: move(3, held(4, q), 3, q, up)),
+        4: (y == 0, lambda q: move(4, held(4, q), 1, q, high)),
+        5: ((y == 1) | (y == 2), lambda q: move(5, held(1, q), 2, q, down)),
+        6: ((y == 1) | (y == 2), lambda q: move(6, held(3, q), 2, q, up)),
+    }
+
+    def act(stream, q, what):
+        cond, make = copies[stream]
+        if cond is None:
+            getattr(make(q), what)()
+        else:
+
+            @pl.when(cond)
+            def _():
+                getattr(make(q), what)()
+
+    def arrived(k, q):
+        move(0, held(k, q), k, q, sibling()).wait_recv()
+        to_sibling(k, q).start()
+
+    for q in range(PIECES):
+        for stream in (0, 1, 2):
+            act(stream, q, "start")
+    for k in range(1, WIDTH + 1):
+        pot_copy(k).start()
+    for q in range(PIECES):
+        arrived(4, q)
+        act(3, q, "start")
+        act(4, q, "start")
+        arrived(1, q)
+        act(5, q, "start")
+    for q in range(PIECES):
+        arrived(3, q)
+        act(6, q, "start")
+    for q in range(PIECES):
+        arrived(2, q)
+    for k in range(1, WIDTH + 1):
+        pot_copy(k).wait()
+    for q in range(PIECES):
+        for stream in range(7):
+            act(stream, q, "wait_send")
+        for k in range(1, WIDTH + 1):
+            to_sibling(k, q).wait()
+
+
+def spread_kernel(boxes, got, sib0, send, recv, dsend, drecv, osend, orecv):
+    core = lax.axis_index("group") % 2
+    greet()
+
+    def part(q):
+        return pl.ds(q * BOXES, BOXES)
+
+    def ship(k, q):
+        return remote(
+            boxes.at[k, part(q)],
+            got.at[k - 1, core, part(q)],
+            send.at[k - 1, q],
+            recv.at[k - 1, q],
+            slab_at(k),
+        )
+
+    def to_sibling(k, q):
+        here = got.at[k - 1, core, part(q)]
+        return remote(here, here, dsend.at[k - 1, q], drecv.at[k - 1, q], sibling())
+
+    first = remote(boxes.at[0], sib0, osend, orecv, sibling())
+    for q in range(SHIPS):
+        for k in (4, 1, 3, 2):
+            ship(k, q).start()
+    first.start()
+    for q in range(SHIPS):
+        for k in (4, 1, 3, 2):
+            ship(k, q).wait_recv()
+            to_sibling(k, q).start()
+    first.wait()
+    for q in range(SHIPS):
+        for k in range(1, WIDTH + 1):
+            ship(k, q).wait_send()
+            to_sibling(k, q).wait()
 
 
 def body(orbitals, potential, box_shift, pair_partner, pair_member):
@@ -322,15 +441,32 @@
     pot = jnp.dot(
         potential, fold.astype(jnp.float32), precision=lax.Precision.HIGHEST
     )
-    half = lax.dynamic_slice_in_dim(own, core * HALF, HALF, 0)
-    mine = jnp.stack([behind(half, k) for k in range(1, WIDTH + 1)])
-    pots = jnp.concatenate([pot] + [behind(pot, k) for k in range(1, WIDTH + 1)], axis=0)
-    sib = swap_cores(mine)
+    smem = pl.BlockSpec(memory_space=pltpu.SMEM)
+    vmem = pl.BlockSpec(memory_space=pltpu.VMEM)
+    anywhere = pl.BlockSpec(memory_space=pl.ANY)
+    dma = pltpu.SemaphoreType.DMA
+    win, potw = pl.pallas_call(
+        fetch_kernel,
+        out_shape=(
+            jax.ShapeDtypeStruct((WIDTH, NCOL, CX, CROSS), jnp.bfloat16),
+            jax.ShapeDtypeStruct((WIDTH, CX, CROSS), jnp.float32),
+        ),
+        in_specs=[anywhere] * 2,
+        out_specs=(anywhere, anywhere),
+        scratch_shapes=[
+            dma((7, PIECES)),
+            dma((WIDTH, PIECES)),
+            dma((WIDTH, PIECES)),
+            dma((WIDTH, PIECES)),
+            dma((WIDTH,)),
+            dma((WIDTH,)),
+        ],
+        compiler_params=pltpu.CompilerParams(collective_id=0, has_side_effects=True),
+        name="fetch",
+    )(own, pot)
     idx = jnp.stack([slab, core])
     partners = lax.dynamic_slice_in_dim(pair_partner, slab * 3, 3, 0).reshape(-1)
     members = lax.dynamic_slice_in_dim(pair_member, slab * 3, 3, 0).reshape(-1)
-    smem = pl.BlockSpec(memory_space=pltpu.SMEM)
-    vmem = pl.BlockSpec(memory_space=pltpu.VMEM)
     boxes = pl.pallas_call(
         solve_kernel,
         out_shape=jax.ShapeDtypeStruct((WIDTH + 1, MINE, CX, CROSS), jnp.float32),
@@ -346,18 +482,29 @@
         + [pltpu.SMEM((SLOTS + BATCH,), jnp.int32)] * 5,
         compiler_params=pltpu.CompilerParams(vmem_limit_bytes=60 * 2**20),
         name="solve",
-    )(idx, box_shift, partners, members, own, mine, sib, pots, ktab, ltab, inv, a3, b3, lx)
-    got = jnp.stack([boxes[0]] + [ahead(boxes[k], k) for k in range(1, WIDTH + 1)])
-    other = swap_cores(got)
+    )(idx, box_shift, partners, members, own, win, pot, potw, ktab, ltab, inv, a3, b3, lx)
+    piece = (MINE, CX, CROSS)
+    got, sib0 = pl.pallas_call(
+        spread_kernel,
+        out_shape=(
+            jax.ShapeDtypeStruct((WIDTH, 2) + piece, jnp.float32),
+            jax.ShapeDtypeStruct(piece, jnp.float32),
+        ),
+        in_specs=[anywhere],
+        out_specs=(anywhere, anywhere),
+        scratch_shapes=[dma((WIDTH, SHIPS))] * 4 + [dma, dma],
+        compiler_params=pltpu.CompilerParams(collective_id=1, has_side_effects=True),
+        name="spread",
+    )(boxes)
     return pl.pallas_call(
         place_kernel,
         out_shape=jax.ShapeDtypeStruct((NCOL, CX, CROSS), jnp.float32),
-        in_specs=[smem] * 2 + [vmem] * 2,
+        in_specs=[smem] * 2 + [vmem] * 3,
         out_specs=vmem,
         scratch_shapes=[pltpu.SMEM((WIDTH,), jnp.int32)],
         compiler_params=pltpu.CompilerParams(vmem_limit_bytes=40 * 2**20),
         name="place",
-    )(idx, box_shift, got, other)
+    )(idx, box_shift, boxes[0], sib0, got)
 
 
 def solution(mesh):

time: 182 us -> 143 us (0.79)
  the two profiles are of different devices: /device:TPU:19 before, /device:TPU:1 now
where the time goes in v1:
time: 143 us; the launch traced here: 141 us
  Pallas kernels  128 us (90%)
  local copies, waits for them, and re-layouts  6.36 us (4%)
  matrix products  6.03 us (4%)
    pallas_call x1, Pallas kernels, body(): pl.pallas_call(fetch_kernel, out_shape=(jax.ShapeDtypeStruct((WIDTH, NCOL...  50.7 us
    pallas_call x1, Pallas kernels, body(): pl.pallas_call(spread_kernel, out_shape=(jax.ShapeDtypeStruct((WIDTH, 2)...  46.5 us
    pallas_call x1, Pallas kernels, body(): pl.pallas_call(solve_kernel, out_shape=jax.ShapeDtypeStruct((WIDTH + 1, M...  24.4 us
    pallas_call x1, Pallas kernels, body(): pl.pallas_call(place_kernel, out_shape=jax.ShapeDtypeStruct((NCOL, CX, CR...  6.15 us
    dot_general x1, matrix products, body(): jnp.dot(orbitals.reshape(NCOL * CX, CROSS), fold, preferred_element_type=...  3.21 us
    unnamed x10, local copies, waits for them, and re-layouts  2.89 us

profile of v1, /device:TPU:1, one launch (start us, length us, event | category | flops | bytes accessed | tf_op | source)
XLA Modules:
  0.0 140.8 jit_solution(13197490987776867726)
XLA Ops:
  0.0 0.0 copy-start
  0.0 0.6 pad_add_fusion.idx_ref
  0.6 2.8 %fusion.8.pot.pot_ref = f32[8,1024]{1,0:T(8,128)} fusion(f32[8,1024]{1,0:T(8,128)} %param.12, s32[1024]{0:T(1024)S(1)} %fusion.17), kind=kOutput, calls=%fused_computation.7 | convolution fusion | flops 101711872 | bytes 69632 | tf_op jit(solution)/shard_map/dot_general | solution.py:441
  3.4 0.9 constant_dynamic-slice_fusion
  4.4 0.1 copy.13
  4.4 0.7 reshape.49.member_ref
  5.1 0.1 copy.12
  5.2 0.7 reshape.48.partner_ref
  5.9 0.0 copy-done
  5.9 3.2 %fusion.5.own.own_ref = bf16[96,8,1024]{2,1,0:T(8,128)(2,1)} fusion(bf16[96,8,1024]{2,1,0:T(8,128)(2,1)S(1)} %copy-done, s32[1024]{0:T(1024)S(1)} %fusion.17), kind=kOutput, calls=%fused_computation.6 | convolution fusion | flops 1611661312 | bytes 3149824 | tf_op jit(solution)/shard_map/dot_general | solution.py:438
  9.1 50.7 %fetch.1 = (bf16[4,96,8,1024]{3,2,1,0:T(8,128)(2,1)}, f32[4,8,1024]{2,1,0:T(8,128)}) custom-call(bf16[96,8,1024]{2,1,0:T(8,128)(2,1)} %fusion.5.own.own_ref, f32[8,1024]{1,0:T(8,128)} %fusion.8.pot.pot_ref), custom_call_target="tpu_custom_call" | custom-call | tf_op jit(solution)/shard_map/fetch/pallas_call | solution.py:448
  59.8 24.4 %solve.1.boxes = f32[5,12,8,1024]{3,2,1,0:T(8,128)} custom-call(s32[2]{0:T(128)} %pad_add_fusion.idx_ref, s32[96]{0:T(128)} %shift_ref.3, s32[168]{0:T(256)} %reshape.48.partner_ref, s32[168]{0:T(256)} %reshape.49.member_ref, bf16[96,8,1024]{2,1,0:T(8,128)(2,1)} %fusion.5.own.own_ref, bf16[4,96,8,1024]{3,2,1,0:T(8,128)(2,1)} %get-tuple-element.9.win_ref, ...), custom_call_target="tpu_custom_call" | custom-call | tf_op jit(solution)/shard_map/solve/pallas_call | solution.py:470
  84.2 0.0 copy-start.3
  84.2 0.0 copy-start.4
  84.2 1.0 slice_bitcast_fusion.mine_ref
  85.2 46.5 %spread.1 = (f32[4,2,12,8,1024]{4,3,2,1,0:T(8,128)}, f32[12,8,1024]{2,1,0:T(8,128)}) custom-call(f32[5,12,8,1024]{3,2,1,0:T(8,128)} %solve.1.boxes), custom_call_target="tpu_custom_call" | custom-call | tf_op jit(solution)/shard_map/spread/pallas_call | solution.py:487
  131.7 0.0 copy-done.3
  131.7 0.0 copy-done.4
  131.8 0.0 copy-start.1
  131.8 1.9 %copy-done.1 = f32[4,2,12,8,1024]{4,3,2,1,0:T(8,128)S(1)} copy-done((f32[4,2,12,8,1024]{4,3,2,1,0:T(8,128)S(1)}, f32[4,2,12,8,1024]{4,3,2,1,0:T(8,128)}, u32[]{:S(2)}) %copy-start.1) | copy-done | bytes 3145752
  133.6 0.0 copy-start.2
  133.6 1.0 copy-done.2
  134.6 6.1 %place.1 = f32[96,8,1024]{2,1,0:T(8,128)} custom-call(s32[2]{0:T(128)S(1)} %copy-done.4, s32[96]{0:T(128)S(1)} %copy-done.3, f32[12,8,1024]{2,1,0:T(8,128)S(1)} %slice_bitcast_fusion.mine_ref, f32[12,8,1024]{2,1,0:T(8,128)S(1)} %copy-done.2, f32[4,2,12,8,1024]{4,3,2,1,0:T(8,128)S(1)} %copy-done.1), custom_call_target="tpu_custom_call" | custom-call | tf_op jit(solution)/shard_map/place/pallas_call | solution.py:499
  (1 shorter events, 0.0 us)
Async XLA Ops:
  0.0 5.9 %copy-start = (bf16[96,8,1024]{2,1,0:T(8,128)(2,1)S(1)}, bf16[96,8,1024]{2,1,0:T(8,128)(2,1)}, u32[]{:S(2)}) copy-start(bf16[96,8,1024]{2,1,0:T(8,128)(2,1)} %param.11) | copy-start | bytes 4718596
  84.2 47.5 %copy-start.3 = (s32[96]{0:T(128)S(1)}, s32[96]{0:T(128)}, u32[]{:S(2)}) copy-start(s32[96]{0:T(128)} %shift_ref.3) | copy-start | bytes 1156
  84.2 47.5 %copy-start.4 = (s32[2]{0:T(128)S(1)}, s32[2]{0:T(128)}, u32[]{:S(2)}) copy-start(s32[2]{0:T(128)} %pad_add_fusion.idx_ref) | copy-start | bytes 28
  131.8 1.9 %copy-start.1 = (f32[4,2,12,8,1024]{4,3,2,1,0:T(8,128)S(1)}, f32[4,2,12,8,1024]{4,3,2,1,0:T(8,128)}, u32[]{:S(2)}) copy-start(f32[4,2,12,8,1024]{4,3,2,1,0:T(8,128)} %get-tuple-element.12.got_ref) | copy-start | bytes 9437188
  133.6 1.0 copy-start.2

commit v2 on v0

v2 whole, which is shorter than its diff:
```python
import functools

import jax
import jax.numpy as jnp
import numpy as np
from jax import lax
from jax.experimental import pallas as pl
from jax.experimental.pallas import tpu as pltpu
from jax.sharding import PartitionSpec as P

B = 32
CX = 8
MEMBERS = 8
NCOL = 96
HALF = NCOL // 2
SLABS = 64
WIDTH = 4
CROSS = B * B
QUAD = CROSS // 4
WIN = (WIDTH + 1) * CX
MINE = 12
BATCH = 8
SLOTS = 168
PIECES = 8
PIECE = HALF // PIECES
SHIPS = 4
BOXES = MINE // SHIPS

lap_weights = (
    -5369.0 / 1800.0,
    12.0 / 7.0,
    -15.0 / 56.0,
    10.0 / 189.0,
    -1.0 / 112.0,
    2.0 / 1925.0,
    -1.0 / 16632.0,
)
stencil_reach = 6
mixing = 0.25


def halves(values):
    hi = values.astype(jnp.bfloat16).astype(np.float64)
    lo = (values - hi).astype(jnp.bfloat16).astype(np.float64)
    return hi, lo


def tables():
    idx = np.arange(1, B + 1)
    sine = np.sqrt(2.0 / (B + 1)) * np.sin(np.pi * np.outer(idx, idx) / (B + 1))
    single = 2.0 - 2.0 * np.cos(np.pi * idx / (B + 1))
    part = [sine[: B // 2, p::2] for p in (0, 1)]
    lap = np.zeros((B, B))
    for o, w in enumerate(lap_weights):
        lap += w * (np.eye(B, k=o) if o == 0 else np.eye(B, k=o) + np.eye(B, k=-o))
    flip = lap[: B // 2, ::-1][:, : B // 2]
    fold = [lap[: B // 2, : B // 2] + flip, lap[: B // 2, : B // 2] - flip]
    eye = np.eye(B // 2)
    kmat, lmat, modes = [], [], []
    for py in (0, 1):
        for pz in (0, 1):
            kmat.append(np.kron(part[py], part[pz]))
            lmat.append(-0.125 * (np.kron(fold[py], eye) + np.kron(eye, fold[pz])).T)
            cross = single[py::2][:, None] + single[pz::2][None, :]
            modes.append(single[:, None] + cross.reshape(1, -1))
    inv = (-mixing / np.concatenate(modes, axis=1)).astype(np.float32)
    ktab = np.stack(halves(np.stack(kmat))).astype(jnp.bfloat16)
    ltab = np.stack(halves(np.stack(lmat))).astype(jnp.bfloat16)
    a3 = np.zeros((CX, B, 128))
    b3 = np.zeros((CX, WIN, 128))
    lx = np.zeros((CX, WIN, 128))
    for sub in range(CX):
        placed = np.zeros((B, WIN))
        placed[:, sub : sub + B] = sine
        hi, lo = halves(placed)
        a3[sub, :, :120] = np.concatenate([hi, hi, lo], axis=1)
        b3[sub, :, :96] = np.concatenate([hi.T, hi.T, lo.T], axis=1)
        lap_placed = np.zeros((WIN, WIN))
        lap_placed[sub : sub + B, sub : sub + B] = -0.5 * lap
        hi, lo = halves(lap_placed)
        lx[sub, :, :80] = np.concatenate([hi, lo], axis=1)
    return (
        ktab,
        ltab,
        inv,
        a3.astype(np.float32),
        b3.astype(np.float32),
        lx.astype(jnp.bfloat16),
    )


def fold_lane(j, hy):
    hz, yp, zp = j // 128, j % 128 // 16, j % 16
    yl = yp if hy == 0 else 7 - yp
    return yl * B + zp + hz * (B - 1 - 2 * zp)


def folding(hy):
    j = lax.broadcasted_iota(jnp.int32, (1, QUAD), 1)
    lanes = lax.broadcasted_iota(jnp.int32, (QUAD, QUAD), 0)
    return jnp.where(lanes == fold_lane(j, hy), 1.0, 0.0).astype(jnp.bfloat16)


def unfolding(hy):
    j = lax.broadcasted_iota(jnp.int32, (QUAD, 1), 0)
    lanes = lax.broadcasted_iota(jnp.int32, (QUAD, QUAD), 1)
    return jnp.where(lanes == fold_lane(j, hy), 1.0, 0.0).astype(jnp.bfloat16)


def chunk_home(n):
    hy = n // 2
    h = n if hy == 0 else 3 - n
    return [slice((hy * 2 + hz) * QUAD + h * 128, (hy * 2 + hz) * QUAD + h * 128 + 128) for hz in (0, 1)]


def butterfly(v):
    q = [v[:, i * QUAD : (i + 1) * QUAD] for i in range(4)]
    sy0, sy1, dy0, dy1 = q[0] + q[2], q[1] + q[3], q[0] - q[2], q[1] - q[3]
    return jnp.concatenate([sy0 + sy1, sy0 - sy1, dy0 + dy1, dy0 - dy1], axis=1)


def split(v):
    hi = v.astype(jnp.bfloat16)
    lo = (v - hi.astype(jnp.float32)).astype(jnp.bfloat16)
    return hi, lo


def dot3(v, hi_mat, lo_mat):
    hi, lo = split(v)
    rows = v.shape[0]
    both = jnp.dot(
        jnp.concatenate([hi, lo], axis=0), hi_mat, preferred_element_type=jnp.float32
    )
    low = jnp.dot(hi, lo_mat, preferred_element_type=jnp.float32)
    return both[:rows] + both[rows:] + low


GROUP = 32


def prep_kernel(orb_ref, pot_ref, own_ref, planes_ref):
    fold = [folding(0), folding(1)]

    def some(g, _):
        x = orb_ref[pl.ds(g * GROUP, GROUP)].astype(jnp.float32)
        x = x.reshape(GROUP * CX, CROSS).astype(jnp.bfloat16)
        for n in range(4):
            y = jnp.dot(
                x[:, n * QUAD : (n + 1) * QUAD],
                fold[n // 2],
                preferred_element_type=jnp.float32,
            )
            for hz, lanes in enumerate(chunk_home(n)):
                part = y[:, hz * 128 : hz * 128 + 128].reshape(GROUP, CX, 128)
                own_ref[pl.ds(g * GROUP, GROUP), :, lanes] = part.astype(jnp.bfloat16)
        return 0

    lax.fori_loop(0, NCOL // GROUP, some, 0)
    rest = pot_ref[...]
    planes = []
    for _ in range(3):
        top = rest.astype(jnp.bfloat16).astype(jnp.float32)
        planes.append(top)
        rest = rest - top
    x = jnp.concatenate(planes + [jnp.zeros_like(rest)], axis=0).astype(jnp.bfloat16)
    for n in range(4):
        y = jnp.dot(
            x[:, n * QUAD : (n + 1) * QUAD], fold[n // 2], preferred_element_type=jnp.float32
        )
        for hz, lanes in enumerate(chunk_home(n)):
            for p in range(4):
                part = y[p * CX : (p + 1) * CX, hz * 128 : hz * 128 + 128]
                planes_ref[p // 2, p % 2, :, lanes] = part.astype(jnp.bfloat16)


def solve_kernel(
    idx_ref, shift_ref, partner_ref, member_ref,
    own_hbm, win_hbm, pot_ref, potw_ref,
    ktab_hbm, ltab_hbm, inv_ref, a3_ref, b3_ref, lx_ref,
    out_ref,
    own_ref, win_ref, ktab_ref, ltab_ref, ktr_ref,
    wv, pots, acc, stg, home, listed, sems,
):
    slab = idx_ref[0]
    core = idx_ref[1]
    loads = [
        pltpu.make_async_copy(own_hbm, own_ref, sems.at[0]),
        *(
            pltpu.make_async_copy(win_hbm.at[k], win_ref.at[k], sems.at[1 + k])
            for k in range(WIDTH)
        ),
        pltpu.make_async_copy(ltab_hbm, ltab_ref, sems.at[WIDTH + 1]),
        pltpu.make_async_copy(ktab_hbm, ktab_ref, sems.at[WIDTH + 2]),
    ]
    for load in loads:
        load.start()

    def find_home(c, count):
        home[count] = c
        return count + jnp.where((shift_ref[c] >> 3) == (slab & 3), 1, 0)

    lax.fori_loop(0, NCOL, find_home, jnp.int32(0), unroll=8)
    base = 256 - slab * CX

    count = jnp.int32(0)
    for t in range(3):
        block = slab * 3 + t

        def list_slot(p, count, t=t, block=block):
            pid = partner_ref[p, block]
            a = t * MEMBERS + member_ref[p, block]
            live = jnp.logical_and(pid >= 0, (a & 1) == core)
            pid = jnp.maximum(pid, 0)
            cj = pid >> 4
            rel = (((pid & 15) << 5) + shift_ref[cj] + base) & 511
            listed[count] = ((rel - 224) << 19) + (cj << 12) + (home[a] << 5) + a
            return count + jnp.where(live, 1, 0)

        count = lax.fori_loop(0, SLOTS // 3, list_slot, count, unroll=8)
    for extra in range(BATCH):
        listed[count + extra] = 1024 << 19

    def pair(n):
        word = listed[n]
        ci = (word >> 5) & 127
        return (word >> 1) & 15, ci, (word >> 12) & 127, shift_ref[ci] & 7, (word >> 19) - 32

    lead = idx_ref[2] * WIDTH * CX
    lead_rows = pl.ds(pl.multiple_of(lead, CX), CX)
    tail_rows = pl.ds(pl.multiple_of(WIDTH * CX - lead, CX), CX)

    def whole(planes):
        f = jnp.float32
        return planes[0, 0].astype(f) + planes[0, 1].astype(f) + planes[1, 0].astype(f)

    pots[lead_rows] = whole(pot_ref)
    pots[tail_rows] = whole(potw_ref.at[WIDTH - 1])
    for k in range(1, WIDTH):
        pots[k * CX : (k + 1) * CX] = whole(potw_ref.at[k - 1])

    def widen(rows, source):
        def one(c, _):
            wv[c, rows] = source[c].astype(jnp.float32)
            return 0

        lax.fori_loop(0, NCOL, one, 0, unroll=4)

    loads[0].wait()
    widen(lead_rows, own_ref)
    for k in range(WIDTH):
        loads[1 + k].wait()
        rows = tail_rows if k == WIDTH - 1 else slice((k + 1) * CX, (k + 2) * CX)
        widen(rows, win_ref.at[k])
    loads[WIDTH + 1].wait()
    loads[WIDTH + 2].wait()
    for h in range(2):
        for q in range(4):
            ktr_ref[h, q] = ktab_ref[h, q].astype(jnp.float32).T.astype(jnp.bfloat16)

    row_ids = lax.broadcasted_iota(jnp.int32, (WIN, 1), 0)

    for group in range(2):
        for j in range(6):
            i = group * 6 + j
            c = home[2 * i + core]
            sub = shift_ref[c] % CX
            inside = jnp.logical_and(row_ids >= sub, row_ids < sub + B)
            w = jnp.where(inside, wv[c], 0.0)
            stg[j * WIN : (j + 1) * WIN] = butterfly(w)
            twice = jnp.concatenate([w, w], axis=0).astype(jnp.bfloat16)
            acc[i] = pots[...] * w + jnp.dot(
                lx_ref[sub][:, :80], twice, preferred_element_type=jnp.float32
            )
        for q in range(4):
            cols = slice(q * QUAD, (q + 1) * QUAD)
            v = stg[0 : 6 * WIN, cols]
            stg[0 : 6 * WIN, cols] = dot3(v, ltab_ref[0, q], ltab_ref[1, q])
        for j in range(6):
            i = group * 6 + j
            acc[i] = acc[i] + butterfly(stg[j * WIN : (j + 1) * WIN])

    lane_ids = lax.broadcasted_iota(jnp.int32, (1, 128), 1)
    lane_row = lane_ids - WIN * jnp.where(lane_ids >= WIN, 1, 0)
    lane_row = lane_row - WIN * jnp.where(lane_ids >= 2 * WIN, 1, 0)

    def batch(b, _):
        for p in range(BATCH):
            _, ci, cj, sub, lo = pair(b * BATCH + p)
            held = jnp.logical_and(lane_row >= lo, lane_row < lo + B)
            left = jnp.where(held, a3_ref[sub], 0.0).astype(jnp.bfloat16)
            dens = wv[ci] * wv[cj]
            hi = dens.astype(jnp.bfloat16).astype(jnp.float32)
            stack = jnp.concatenate(
                [hi, dens - hi, hi, jnp.zeros((CX, CROSS), jnp.float32)], axis=0
            ).astype(jnp.bfloat16)
            u = jnp.dot(left, stack, preferred_element_type=jnp.float32)
            stg[p * B : (p + 1) * B] = butterfly(u)
        for q in range(4):
            cols = slice(q * QUAD, (q + 1) * QUAD)
            g = dot3(stg[:, cols], ktab_ref[0, q], ktab_ref[1, q])
            g = g.reshape(BATCH, B, QUAD) * inv_ref[:, cols][None]
            g = g.reshape(BATCH * B, QUAD)
            stg[:, cols] = dot3(g, ktr_ref[0, q], ktr_ref[1, q])
        for p in range(BATCH):
            m, _, cj, sub, lo = pair(b * BATCH + p)
            held = jnp.logical_and(row_ids >= lo, row_ids < lo + B)
            right = jnp.where(held, b3_ref[sub], 0.0).astype(jnp.bfloat16)
            hi, low = split(butterfly(stg[p * B : (p + 1) * B]))
            stack = jnp.concatenate([hi, low, hi], axis=0)
            field = jnp.dot(right[:, :96], stack, preferred_element_type=jnp.float32)
            acc[m] = acc[m] + field * wv[cj]
        return 0

    lax.fori_loop(0, (count + BATCH - 1) // BATCH, batch, 0)

    for n in range(4):
        back = unfolding(n // 2)
        low_z, high_z = chunk_home(n)
        for group in range(2):
            rows = slice(group * 6, group * 6 + 6)
            v = jnp.concatenate([acc[rows, :, low_z], acc[rows, :, high_z]], axis=2)
            hi, lo = split(v.reshape(6 * WIN, QUAD))
            y = jnp.dot(
                jnp.concatenate([hi, lo], axis=0), back, preferred_element_type=jnp.float32
            )
            y = y[: 6 * WIN] + y[6 * WIN :]
            for j in range(6):
                for k in range(WIDTH + 1):
                    first = j * WIN + k * CX
                    out_ref[k, group * 6 + j, :, n * QUAD : (n + 1) * QUAD] = y[
                        first : first + CX
                    ]


def slab_at(step):
    s = lax.axis_index("orb")
    group = lax.axis_index("group")
    y, zl, zh, core = s % 4, (s // 4) % 4, group // 2, group % 2
    if step > 0:
        turn = (zl + (y + step) // 4) // 4
    else:
        turn = 1 - (zl - (1 - (y + step + 4) // 4) + 4) // 4
    return ((zh + turn) % 2 * 2 + core, (s + step + SLABS) % SLABS)


def ring(step):
    s = lax.axis_index("orb")
    return (lax.axis_index("group"), s - s % 4 + (s % 4 + step + 4) % 4)


def either(which, first, second):
    return tuple(a + which * (b - a) for a, b in zip(first, second))


def sibling():
    group = lax.axis_index("group")
    return (group // 2 * 2 + 1 - group % 2, lax.axis_index("orb"))


def greet(others):
    barrier = pltpu.get_barrier_semaphore()
    for other in others:
        pl.semaphore_signal(
            barrier, inc=1, device_id=other, device_id_type=pl.DeviceIdType.MESH
        )
    pl.semaphore_wait(barrier, len(others))


def remote(src, dst, send, recv, device):
    return pltpu.make_async_remote_copy(
        src_ref=src,
        dst_ref=dst,
        send_sem=send,
        recv_sem=recv,
        device_id=device,
        device_id_type=pl.DeviceIdType.MESH,
    )


def fetch_kernel(own, pot, win, potw, send, recv, dsend, drecv):
    core = lax.axis_index("group") % 2
    y = lax.axis_index("orb") % 4
    high, odd = y // 2, y % 2
    greet([ring(-1), ring(1), slab_at(-4), slab_at(4), sibling()])

    def mine(q):
        return pot.at[core] if q == PIECES else own.at[pl.ds(core * HALF + q * PIECE, PIECE)]

    def held(t, q):
        if q == PIECES:
            return potw.at[t, core]
        return win.at[t, pl.ds(core * HALF + q * PIECE, PIECE)]

    def move(stream, src, t, q, device):
        return remote(src, held(t, q), send.at[stream, q], recv.at[t, q], device)

    def to_sibling(t, q):
        return remote(held(t, q), held(t, q), dsend.at[t, q], drecv.at[t, q], sibling())

    relayed = 2 - 2 * odd
    onward = either(odd, ring(1), ring(-1))
    copies = {
        0: (None, lambda q: move(0, mine(q), 3, q, either(high, slab_at(-4), slab_at(4)))),
        1: (y != 3, lambda q: move(1, mine(q), 0, q, ring(-1))),
        2: (y == 3, lambda q: move(1, held(3, q), 0, q, ring(-1))),
        3: (y != 0, lambda q: move(2, mine(q), 2, q, ring(1))),
        4: (y == 0, lambda q: move(2, held(3, q), 2, q, ring(1))),
        5: (None, lambda q: move(3, held(relayed, q), 1, q, onward)),
    }

    def act(which, q, what):
        cond, make = copies[which]
        if cond is None:
            getattr(make(q), what)()
        else:

            @pl.when(cond)
            def _():
                getattr(make(q), what)()

    def arrived(t, q):
        move(0, held(t, q), t, q, sibling()).wait_recv()
        to_sibling(t, q).start()

    turns = range(PIECES + 1)
    for q in turns:
        for which in (0, 1, 3):
            act(which, q, "start")
    for q in turns:
        arrived(3, q)
        act(2, q, "start")
        act(4, q, "start")
        arrived(relayed, q)
        act(5, q, "start")
    for q in turns:
        arrived(2 - relayed, q)
    for q in turns:
        arrived(1, q)
    for q in turns:
        for which in range(6):
            act(which, q, "wait_send")
        for t in range(WIDTH):
            to_sibling(t, q).wait()


def spread_kernel(
    shift_ref, boxes, out, got, ext, stage,
    send, recv, rsend, rrecv, dsend, drecv, osend, orecv, ksem,
):
    core = lax.axis_index("group") % 2
    slab = lax.axis_index("orb")
    y = slab % 4
    high, odd = y // 2, y % 2
    greet(
        [ring(-1), ring(1), slab_at(-4), slab_at(4), slab_at(-3), slab_at(3), sibling()]
    )

    def part(q):
        return pl.ds(q * BOXES, BOXES)

    def ship(t, src, q, device):
        return remote(
            src, got.at[t, core, part(q)], send.at[t, q], recv.at[t, q], device
        )

    low_cross = (y % 2) * (1 - high)
    high_cross = (1 - y % 2) * high
    to_one = either(high_cross, ring(1), slab_at(-3))
    to_three = either(low_cross, ring(-1), slab_at(3))
    to_z = either(high, slab_at(4), slab_at(-4))
    outer = WIDTH * (1 - high)
    inner = WIDTH * high

    def by_z(q):
        return ship(3, boxes.at[outer, part(q)], q, to_z)

    def by_one(q):
        return ship(0, boxes.at[1, part(q)], q, to_one)

    def by_three(q):
        return ship(2, boxes.at[3, part(q)], q, to_three)

    def to_relay(q):
        return remote(
            boxes.at[2, part(q)],
            stage.at[part(q)],
            rsend.at[q],
            rrecv.at[q],
            either(odd, ring(1), ring(-1)),
        )

    def relay(q):
        return ship(1, stage.at[part(q)], q, either(odd, ring(-1), ring(1)))

    def to_sibling(t, q):
        here = got.at[t, core, part(q)]
        return remote(here, here, dsend.at[t, q], drecv.at[t, q], sibling())

    def arrived(t, q):
        ship(t, boxes.at[0, part(q)], q, sibling()).wait_recv()
        to_sibling(t, q).start()

    local = remote(boxes.at[inner], ext.at[core], osend, orecv, sibling())
    for q in range(SHIPS):
        to_relay(q).start()
    for q in range(SHIPS):
        by_z(q).start()
        by_one(q).start()
        by_three(q).start()
    local.start()
    keep = pltpu.make_async_copy(boxes.at[inner], ext.at[core], ksem)
    keep.start()
    for q in range(SHIPS):
        to_relay(q).wait_recv()
        relay(q).start()
    for q in range(SHIPS):
        arrived(3, q)
        arrived(0, q)
        arrived(2, q)
    for q in range(SHIPS):
        arrived(1, q)
    local.wait()
    keep.wait()
    for q in range(SHIPS):
        to_relay(q).wait_send()
        for copy in (by_z(q), by_one(q), by_three(q), relay(q)):
            copy.wait_send()
        for t in range(WIDTH):
            to_sibling(t, q).wait()

    def place(c, ranks):
        cl = shift_ref[c] // CX
        a = sum(jnp.where(cl == n, rank, 0) for n, rank in enumerate(ranks))
        a = jnp.minimum(a, 2 * MINE - 1)
        k = (slab - cl + SLABS) % 4
        t = jnp.where(k == 0, WIDTH - 1, k - 1)
        extra = jnp.where(k == 0, 1.0, 0.0)
        out[c] = got[t, a % 2, a // 2] + extra * ext[a % 2, a // 2]
        return tuple(rank + jnp.where(cl == n, 1, 0) for n, rank in enumerate(ranks))

    lax.fori_loop(0, NCOL, place, (jnp.int32(0),) * WIDTH, unroll=4)


def body(orbitals, potential, box_shift, pair_partner, pair_member):
    ktab, ltab, inv, a3, b3, lx = tables()
    place = lax.axis_index("orb").astype(jnp.int32)
    high = place % 4 // 2
    slab = (place - 4 * high) % SLABS
    core = lax.axis_index("group").astype(jnp.int32) % 2
    smem = pl.BlockSpec(memory_space=pltpu.SMEM)
    vmem = pl.BlockSpec(memory_space=pltpu.VMEM)
    hbm = pl.BlockSpec(memory_space=pltpu.HBM)
    dma = pltpu.SemaphoreType.DMA
    own, pot = pl.pallas_call(
        prep_kernel,
        out_shape=(
            jax.ShapeDtypeStruct((NCOL, CX, CROSS), jnp.bfloat16),
            jax.ShapeDtypeStruct((2, 2, CX, CROSS), jnp.bfloat16),
        ),
        in_specs=[vmem] * 2,
        out_specs=(vmem, vmem),
        name="prep",
    )(orbitals, potential)
    streams = (WIDTH, PIECES + 1)
    win, potw = pl.pallas_call(
        fetch_kernel,
        out_shape=(
            jax.ShapeDtypeStruct((WIDTH, NCOL, CX, CROSS), jnp.bfloat16),
            jax.ShapeDtypeStruct((WIDTH, 2, 2, CX, CROSS), jnp.bfloat16),
        ),
        in_specs=[hbm] * 2,
        out_specs=(hbm, hbm),
        scratch_shapes=[dma(streams)] * 4,
        compiler_params=pltpu.CompilerParams(collective_id=0, has_side_effects=True),
        name="fetch",
    )(own, pot)
    idx = jnp.stack([slab, core, high])
    boxes = pl.pallas_call(
        solve_kernel,
        out_shape=jax.ShapeDtypeStruct((WIDTH + 1, MINE, CX, CROSS), jnp.float32),
        in_specs=[smem] * 4 + [hbm] * 2 + [vmem] * 2 + [hbm] * 2 + [vmem] * 4,
        out_specs=vmem,
        scratch_shapes=[
            pltpu.VMEM((NCOL, CX, CROSS), jnp.bfloat16),
            pltpu.VMEM((WIDTH, NCOL, CX, CROSS), jnp.bfloat16),
        ]
        + [pltpu.VMEM((2, 4, QUAD, QUAD), jnp.bfloat16)] * 3
        + [
            pltpu.VMEM((NCOL, WIN, CROSS), jnp.float32),
            pltpu.VMEM((WIN, CROSS), jnp.float32),
            pltpu.VMEM((MINE, WIN, CROSS), jnp.float32),
            pltpu.VMEM((BATCH * B, CROSS), jnp.float32),
            pltpu.SMEM((32,), jnp.int32),
        ]
        + [pltpu.SMEM((SLOTS + BATCH,), jnp.int32)]
        + [dma((WIDTH + 3,))],
        compiler_params=pltpu.CompilerParams(vmem_limit_bytes=60 * 2**20),
        name="solve",
    )(idx, box_shift, pair_partner.T, pair_member.T, own, win, pot, potw, ktab, ltab, inv, a3, b3, lx)
    piece = (MINE, CX, CROSS)
    ships = (WIDTH, SHIPS)
    return pl.pallas_call(
        spread_kernel,
        out_shape=jax.ShapeDtypeStruct((NCOL, CX, CROSS), jnp.float32),
        in_specs=[smem, hbm],
        out_specs=vmem,
        scratch_shapes=[
            pltpu.VMEM((WIDTH, 2) + piece, jnp.float32),
            pltpu.VMEM((2,) + piece, jnp.float32),
            pltpu.VMEM(piece, jnp.float32),
            dma(ships),
            dma(ships),
            dma((SHIPS,)),
            dma((SHIPS,)),
            dma(ships),
            dma(ships),
            dma,
            dma,
            dma,
        ],
        compiler_params=pltpu.CompilerParams(
            collective_id=1, has_side_effects=True, vmem_limit_bytes=40 * 2**20
        ),
        name="spread",
    )(box_shift, boxes)


def solution(mesh):
    placed = (P(None, "orb", None), P("orb", None), P(), P(), P())
    return jax.shard_map(
        body, mesh=mesh, in_specs=placed, out_specs=P(None, "orb", None), check_vma=False
    )
```

time: 182 us -> 112 us (0.62)
  the two profiles are of different devices: /device:TPU:19 before, /device:TPU:5 now
where the time goes in v2:
time: 112 us
  Pallas kernels  109 us (97%)
  local copies, waits for them, and re-layouts  3.21 us (3%)
    pallas_call x1, Pallas kernels, body(): pl.pallas_call(fetch_kernel, out_shape=(jax.ShapeDtypeStruct((WIDTH, NCOL...  46.3 us
    pallas_call x1, Pallas kernels, body(): pl.pallas_call(spread_kernel, out_shape=jax.ShapeDtypeStruct((NCOL, CX, C...  38.8 us
    pallas_call x1, Pallas kernels, body(): pl.pallas_call(solve_kernel, out_shape=jax.ShapeDtypeStruct((WIDTH + 1, M...  19.9 us
    pallas_call x1, Pallas kernels, body(): pl.pallas_call(prep_kernel, out_shape=(jax.ShapeDtypeStruct((NCOL, CX, CR...  3.57 us
    unnamed x5, local copies, waits for them, and re-layouts  3.21 us

profile of v2, /device:TPU:5, one launch (start us, length us, event | category | flops | bytes accessed | tf_op | source)
XLA Modules:
  0.0 112.3 jit_solution(4106576533454233949)
XLA Ops:
  0.0 0.6 pad_add_fusion.idx_ref
  0.6 3.6 %prep.1 = (bf16[96,8,1024]{2,1,0:T(8,128)(2,1)}, bf16[2,2,8,1024]{3,2,1,0:T(8,128)(2,1)}) custom-call(bf16[96,8,1024]{2,1,0:T(8,128)(2,1)} %orb_ref.1, f32[8,1024]{1,0:T(8,128)} %pot_ref.1), custom_call_target="tpu_custom_call" | custom-call | tf_op jit(solution)/shard_map/prep/pallas_call | solution.py:554
  4.1 46.3 %fetch.1 = (bf16[4,96,8,1024]{3,2,1,0:T(8,128)(2,1)}, bf16[4,2,2,8,1024]{4,3,2,1,0:T(8,128)(2,1)}) custom-call(bf16[96,8,1024]{2,1,0:T(8,128)(2,1)} %get-tuple-element.9.own.own_hbm, bf16[2,2,8,1024]{3,2,1,0:T(8,128)(2,1)} %get-tuple-element.10.pot.pot_ref), custom_call_target="tpu_custom_call" | custom-call | tf_op jit(solution)/shard_map/fetch/pallas_call | solution.py:565
  50.4 0.0 copy-start.1
  50.4 19.9 %solve.1.boxes = f32[5,12,8,1024]{3,2,1,0:T(8,128)} custom-call(s32[3]{0:T(128)} %pad_add_fusion.idx_ref, s32[96]{0:T(128)} %shift_ref.3, s32[56,192]{1,0:T(8,128)} %bitcast.5, s32[56,192]{1,0:T(8,128)} %bitcast.6, bf16[96,8,1024]{2,1,0:T(8,128)(2,1)} %get-tuple-element.9.own.own_hbm, bf16[4,96,8,1024]{3,2,1,0:T(8,128)(2,1)} %get-tuple-element.11.win_hbm, ...), custom_call_target="tpu_custom_call" | custom-call | tf_op jit(solution)/shard_map/solve/pallas_call | solution.py:578
  70.3 0.0 copy-done.1
  70.4 0.0 copy-start
  70.4 1.5 %copy-done = f32[5,12,8,1024]{3,2,1,0:T(8,128)S(1)} copy-done((f32[5,12,8,1024]{3,2,1,0:T(8,128)S(1)}, f32[5,12,8,1024]{3,2,1,0:T(8,128)}, u32[]{:S(2)}) %copy-start) | copy-done | bytes 1966104
  71.9 38.8 %spread.1 = f32[96,8,1024]{2,1,0:T(8,128)S(1)} custom-call(s32[96]{0:T(128)S(1)} %copy-done.1, f32[5,12,8,1024]{3,2,1,0:T(8,128)S(1)} %copy-done), custom_call_target="tpu_custom_call" | custom-call | tf_op jit(solution)/shard_map/spread/pallas_call | solution.py:602
  110.7 1.7 %copy.13 = f32[96,8,1024]{2,1,0:T(8,128)} copy(f32[96,8,1024]{2,1,0:T(8,128)S(1)} %spread.1) | data formatting | bytes 6291456
Async XLA Ops:
  50.4 19.9 %copy-start.1 = (s32[96]{0:T(128)S(1)}, s32[96]{0:T(128)}, u32[]{:S(2)}) copy-start(s32[96]{0:T(128)} %shift_ref.3) | copy-start | bytes 1156
  70.4 1.5 %copy-start = (f32[5,12,8,1024]{3,2,1,0:T(8,128)S(1)}, f32[5,12,8,1024]{3,2,1,0:T(8,128)}, u32[]{:S(2)}) copy-start(f32[5,12,8,1024]{3,2,1,0:T(8,128)} %solve.1.boxes) | copy-start | bytes 5898244

commit v3 on v2

--- a/solution.py
+++ b/solution.py
@@ -135,49 +135,46 @@
     return both[:rows] + both[rows:] + low
 
 
-GROUP = 32
-
-
-def prep_kernel(orb_ref, pot_ref, own_ref, planes_ref):
-    fold = [folding(0), folding(1)]
-
-    def some(g, _):
-        x = orb_ref[pl.ds(g * GROUP, GROUP)].astype(jnp.float32)
-        x = x.reshape(GROUP * CX, CROSS).astype(jnp.bfloat16)
+GROUP = 16
+
+
+def prep_kernel(orb_ref, pot_ref, own_ref, planes_ref, fold):
+    @pl.when(pl.program_id(0) == 0)
+    def _():
+        fold[0] = folding(0)
+        fold[1] = folding(1)
+        rest = pot_ref[...]
+        planes = []
+        for _ in range(3):
+            top = rest.astype(jnp.bfloat16).astype(jnp.float32)
+            planes.append(top)
+            rest = rest - top
+        x = jnp.concatenate(planes + [jnp.zeros_like(rest)], axis=0).astype(jnp.bfloat16)
         for n in range(4):
             y = jnp.dot(
-                x[:, n * QUAD : (n + 1) * QUAD],
-                fold[n // 2],
-                preferred_element_type=jnp.float32,
+                x[:, n * QUAD : (n + 1) * QUAD], fold[n // 2], preferred_element_type=jnp.float32
             )
             for hz, lanes in enumerate(chunk_home(n)):
-                part = y[:, hz * 128 : hz * 128 + 128].reshape(GROUP, CX, 128)
-                own_ref[pl.ds(g * GROUP, GROUP), :, lanes] = part.astype(jnp.bfloat16)
-        return 0
-
-    lax.fori_loop(0, NCOL // GROUP, some, 0)
-    rest = pot_ref[...]
-    planes = []
-    for _ in range(3):
-        top = rest.astype(jnp.bfloat16).astype(jnp.float32)
-        planes.append(top)
-        rest = rest - top
-    x = jnp.concatenate(planes + [jnp.zeros_like(rest)], axis=0).astype(jnp.bfloat16)
+                for p in range(4):
+                    part = y[p * CX : (p + 1) * CX, hz * 128 : hz * 128 + 128]
+                    planes_ref[p // 2, p % 2, :, lanes] = part.astype(jnp.bfloat16)
+
+    x = orb_ref[...].astype(jnp.float32)
+    x = x.reshape(GROUP * CX, CROSS).astype(jnp.bfloat16)
     for n in range(4):
         y = jnp.dot(
             x[:, n * QUAD : (n + 1) * QUAD], fold[n // 2], preferred_element_type=jnp.float32
         )
         for hz, lanes in enumerate(chunk_home(n)):
-            for p in range(4):
-                part = y[p * CX : (p + 1) * CX, hz * 128 : hz * 128 + 128]
-                planes_ref[p // 2, p % 2, :, lanes] = part.astype(jnp.bfloat16)
+            part = y[:, hz * 128 : hz * 128 + 128].reshape(GROUP, CX, 128)
+            own_ref[:, :, lanes] = part.astype(jnp.bfloat16)
 
 
 def solve_kernel(
     idx_ref, shift_ref, partner_ref, member_ref,
     own_hbm, win_hbm, pot_ref, potw_ref,
     ktab_hbm, ltab_hbm, inv_ref, a3_ref, b3_ref, lx_ref,
-    out_ref,
+    out_ref, table_ref,
     own_ref, win_ref, ktab_ref, ltab_ref, ktr_ref,
     wv, pots, acc, stg, home, listed, sems,
 ):
@@ -195,11 +192,18 @@
     for load in loads:
         load.start()
 
-    def find_home(c, count):
-        home[count] = c
-        return count + jnp.where((shift_ref[c] >> 3) == (slab & 3), 1, 0)
-
-    lax.fori_loop(0, NCOL, find_home, jnp.int32(0), unroll=8)
+    def rank_colour(c, ranks):
+        cl = shift_ref[c] >> 3
+        a = sum(jnp.where(cl == n, rank, 0) for n, rank in enumerate(ranks))
+        k = (slab - cl) & 3
+        near = jnp.where(k == 0, 1, 0)
+        box = (a & 1) * MINE + (a >> 1)
+        t = ((k + 3) & 3) * 2 * MINE
+        table_ref[c] = t + box + (box << 7) + (near << 12)
+        home[jnp.where(k == 0, a, 31)] = c
+        return tuple(rank + jnp.where(cl == n, 1, 0) for n, rank in enumerate(ranks))
+
+    lax.fori_loop(0, NCOL, rank_colour, (jnp.int32(0),) * WIDTH, unroll=4)
     base = 256 - slab * CX
 
     count = jnp.int32(0)
@@ -444,7 +448,7 @@
 
 
 def spread_kernel(
-    shift_ref, boxes, out, got, ext, stage,
+    table_ref, boxes, out, got, ext, stage,
     send, recv, rsend, rrecv, dsend, drecv, osend, orecv, ksem,
 ):
     core = lax.axis_index("group") % 2
@@ -458,10 +462,11 @@
     def part(q):
         return pl.ds(q * BOXES, BOXES)
 
+    def landing(t, q):
+        return got.at[pl.ds((t * 2 + core) * MINE + q * BOXES, BOXES)]
+
     def ship(t, src, q, device):
-        return remote(
-            src, got.at[t, core, part(q)], send.at[t, q], recv.at[t, q], device
-        )
+        return remote(src, landing(t, q), send.at[t, q], recv.at[t, q], device)
 
     low_cross = (y % 2) * (1 - high)
     high_cross = (1 - y % 2) * high
@@ -493,14 +498,14 @@
         return ship(1, stage.at[part(q)], q, either(odd, ring(-1), ring(1)))
 
     def to_sibling(t, q):
-        here = got.at[t, core, part(q)]
+        here = landing(t, q)
         return remote(here, here, dsend.at[t, q], drecv.at[t, q], sibling())
 
     def arrived(t, q):
         ship(t, boxes.at[0, part(q)], q, sibling()).wait_recv()
         to_sibling(t, q).start()
 
-    local = remote(boxes.at[inner], ext.at[core], osend, orecv, sibling())
+    local = remote(boxes.at[inner], ext.at[pl.ds(core * MINE, MINE)], osend, orecv, sibling())
     for q in range(SHIPS):
         to_relay(q).start()
     for q in range(SHIPS):
@@ -508,7 +513,7 @@
         by_one(q).start()
         by_three(q).start()
     local.start()
-    keep = pltpu.make_async_copy(boxes.at[inner], ext.at[core], ksem)
+    keep = pltpu.make_async_copy(boxes.at[inner], ext.at[pl.ds(core * MINE, MINE)], ksem)
     keep.start()
     for q in range(SHIPS):
         to_relay(q).wait_recv()
@@ -528,17 +533,13 @@
         for t in range(WIDTH):
             to_sibling(t, q).wait()
 
-    def place(c, ranks):
-        cl = shift_ref[c] // CX
-        a = sum(jnp.where(cl == n, rank, 0) for n, rank in enumerate(ranks))
-        a = jnp.minimum(a, 2 * MINE - 1)
-        k = (slab - cl + SLABS) % 4
-        t = jnp.where(k == 0, WIDTH - 1, k - 1)
-        extra = jnp.where(k == 0, 1.0, 0.0)
-        out[c] = got[t, a % 2, a // 2] + extra * ext[a % 2, a // 2]
-        return tuple(rank + jnp.where(cl == n, 1, 0) for n, rank in enumerate(ranks))
-
-    lax.fori_loop(0, NCOL, place, (jnp.int32(0),) * WIDTH, unroll=4)
+    def place(c, _):
+        word = table_ref[c]
+        extra = jnp.where((word >> 12) == 1, 1.0, 0.0)
+        out[c] = got[word & 127] + extra * ext[(word >> 7) & 31]
+        return 0
+
+    lax.fori_loop(0, NCOL, place, 0, unroll=8)
 
 
 def body(orbitals, potential, box_shift, pair_partner, pair_member):
@@ -557,8 +558,16 @@
             jax.ShapeDtypeStruct((NCOL, CX, CROSS), jnp.bfloat16),
             jax.ShapeDtypeStruct((2, 2, CX, CROSS), jnp.bfloat16),
         ),
-        in_specs=[vmem] * 2,
-        out_specs=(vmem, vmem),
+        grid=(NCOL // GROUP,),
+        in_specs=[
+            pl.BlockSpec((GROUP, CX, CROSS), lambda g: (g, 0, 0)),
+            pl.BlockSpec((CX, CROSS), lambda g: (0, 0)),
+        ],
+        out_specs=(
+            pl.BlockSpec((GROUP, CX, CROSS), lambda g: (g, 0, 0)),
+            pl.BlockSpec((2, 2, CX, CROSS), lambda g: (0, 0, 0, 0)),
+        ),
+        scratch_shapes=[pltpu.VMEM((2, QUAD, QUAD), jnp.bfloat16)],
         name="prep",
     )(orbitals, potential)
     streams = (WIDTH, PIECES + 1)
@@ -575,11 +584,14 @@
         name="fetch",
     )(own, pot)
     idx = jnp.stack([slab, core, high])
-    boxes = pl.pallas_call(
+    boxes, table = pl.pallas_call(
         solve_kernel,
-        out_shape=jax.ShapeDtypeStruct((WIDTH + 1, MINE, CX, CROSS), jnp.float32),
+        out_shape=(
+            jax.ShapeDtypeStruct((WIDTH + 1, MINE, CX, CROSS), jnp.float32),
+            jax.ShapeDtypeStruct((NCOL,), jnp.int32),
+        ),
         in_specs=[smem] * 4 + [hbm] * 2 + [vmem] * 2 + [hbm] * 2 + [vmem] * 4,
-        out_specs=vmem,
+        out_specs=(vmem, smem),
         scratch_shapes=[
             pltpu.VMEM((NCOL, CX, CROSS), jnp.bfloat16),
             pltpu.VMEM((WIDTH, NCOL, CX, CROSS), jnp.bfloat16),
@@ -594,7 +606,7 @@
         ]
         + [pltpu.SMEM((SLOTS + BATCH,), jnp.int32)]
         + [dma((WIDTH + 3,))],
-        compiler_params=pltpu.CompilerParams(vmem_limit_bytes=60 * 2**20),
+        compiler_params=pltpu.CompilerParams(vmem_limit_bytes=44 * 2**20),
         name="solve",
     )(idx, box_shift, pair_partner.T, pair_member.T, own, win, pot, potw, ktab, ltab, inv, a3, b3, lx)
     piece = (MINE, CX, CROSS)
@@ -605,8 +617,8 @@
         in_specs=[smem, hbm],
         out_specs=vmem,
         scratch_shapes=[
-            pltpu.VMEM((WIDTH, 2) + piece, jnp.float32),
-            pltpu.VMEM((2,) + piece, jnp.float32),
+            pltpu.VMEM((WIDTH * 2 * MINE, CX, CROSS), jnp.float32),
+            pltpu.VMEM((2 * MINE, CX, CROSS), jnp.float32),
             pltpu.VMEM(piece, jnp.float32),
             dma(ships),
             dma(ships),
@@ -622,7 +634,7 @@
             collective_id=1, has_side_effects=True, vmem_limit_bytes=40 * 2**20
         ),
         name="spread",
-    )(box_shift, boxes)
+    )(table, boxes)
 
 
 def solution(mesh):

time: 112 us -> 115 us (1.027)
  the two profiles are of different devices: /device:TPU:5 before, /device:TPU:1 now
where the time goes in v3:
time: 115 us; the launch traced here: 113 us
  Pallas kernels  108 us (94%)
  local copies, waits for them, and re-layouts  4.9 us (4%)
    pallas_call x1, Pallas kernels, body(): pl.pallas_call(fetch_kernel, out_shape=(jax.ShapeDtypeStruct((WIDTH, NCOL...  49.3 us
    pallas_call x1, Pallas kernels, body(): pl.pallas_call(spread_kernel, out_shape=jax.ShapeDtypeStruct((NCOL, CX, C...  39.4 us
    pallas_call x1, Pallas kernels, body(): pl.pallas_call(solve_kernel, out_shape=(jax.ShapeDtypeStruct((WIDTH + 1,...  13.6 us
    pallas_call x1, Pallas kernels, body(): pl.pallas_call(prep_kernel, out_shape=(jax.ShapeDtypeStruct((NCOL, CX, CR...  5.52 us
    unnamed x25, local copies, waits for them, and re-layouts  4.9 us

profile of v3, /device:TPU:1, one launch (start us, length us, event | category | flops | bytes accessed | tf_op | source)
XLA Modules:
  0.0 113.1 jit_solution(4883355489242535018)
XLA Ops:
  0.0 0.0 copy-start.8
  0.0 0.0 copy-start.5
  0.0 0.0 copy-start.6
  0.0 0.0 copy-start.7
  0.0 0.0 copy-start.1
  0.0 0.0 copy-start.2
  0.0 0.0 copy-start.10
  0.1 0.0 copy-start.9
  0.1 0.0 copy-start.11
  0.1 0.1 pad_add_fusion.idx_ref
  0.2 5.5 %prep.1 = (bf16[96,8,1024]{2,1,0:T(8,128)(2,1)}, bf16[2,2,8,1024]{3,2,1,0:T(8,128)(2,1)}) custom-call(bf16[96,8,1024]{2,1,0:T(8,128)(2,1)} %orb_ref.1, f32[8,1024]{1,0:T(8,128)} %pot_ref.1), custom_call_target="tpu_custom_call" | custom-call | tf_op jit(solution)/shard_map/prep/pallas_call | solution.py:555
  5.7 49.3 %fetch.1 = (bf16[4,96,8,1024]{3,2,1,0:T(8,128)(2,1)}, bf16[4,2,2,8,1024]{4,3,2,1,0:T(8,128)(2,1)}) custom-call(bf16[96,8,1024]{2,1,0:T(8,128)(2,1)} %get-tuple-element.11.own.own_hbm, bf16[2,2,8,1024]{3,2,1,0:T(8,128)(2,1)} %get-tuple-element.12.pot.pot_ref), custom_call_target="tpu_custom_call" | custom-call | tf_op jit(solution)/shard_map/fetch/pallas_call | solution.py:574
  55.1 0.0 copy-done.8
  55.1 0.0 copy-done.5
  55.1 0.0 copy-done.6
  55.1 0.0 copy-done.7
  55.1 0.0 copy-done.1
  55.1 0.0 copy-done.2
  55.1 0.0 copy-done.10
  55.1 0.0 copy-done.9
  55.1 0.0 copy-done.11
  55.1 0.0 copy-start
  55.2 1.4 %copy-done = bf16[96,8,1024]{2,1,0:T(8,128)(2,1)S(1)} copy-done((bf16[96,8,1024]{2,1,0:T(8,128)(2,1)S(1)}, bf16[96,8,1024]{2,1,0:T(8,128)(2,1)}, u32[]{:S(2)}) %copy-start) | copy-done | bytes 1572888
  56.6 0.0 copy-start.3
  56.6 0.8 copy-done.3
  57.4 0.0 copy-start.4
  57.4 0.9 copy-done.4
  58.3 13.6 %solve.1 = (f32[5,12,8,1024]{3,2,1,0:T(8,128)S(1)}, s32[96]{0:T(128)S(1)}) custom-call(s32[3]{0:T(128)S(1)} %pad_add_fusion.idx_ref, s32[96]{0:T(128)S(1)} %copy-done.11, s32[56,192]{1,0:T(8,128)S(1)} %bitcast.5, s32[56,192]{1,0:T(8,128)S(1)} %bitcast.6, bf16[96,8,1024]{2,1,0:T(8,128)(2,1)S(1)} %copy-done, ...), custom_call_target="tpu_custom_call" | custom-call | tf_op jit(solution)/shard_map/solve/pallas_call | solution.py:587
  72.0 39.4 %spread.1 = f32[96,8,1024]{2,1,0:T(8,128)S(1)} custom-call(s32[96]{0:T(128)S(1)} %get-tuple-element.15.table_ref, f32[5,12,8,1024]{3,2,1,0:T(8,128)S(1)} %get-tuple-element.16.boxes), custom_call_target="tpu_custom_call" | custom-call | tf_op jit(solution)/shard_map/spread/pallas_call | solution.py:614
  111.4 1.7 %copy.13 = f32[96,8,1024]{2,1,0:T(8,128)} copy(f32[96,8,1024]{2,1,0:T(8,128)S(1)} %spread.1) | data formatting | bytes 6291456
Async XLA Ops:
  0.0 55.1 %copy-start.8 = (bf16[8,40,128]{2,1,0:T(8,128)(2,1)S(1)}, bf16[8,40,128]{2,1,0:T(8,128)(2,1)}, u32[]{:S(2)}) copy-start(bf16[8,40,128]{2,1,0:T(8,128)(2,1)} %constant.70.clone.lx_ref) | copy-start | bytes 245764
  0.0 55.1 %copy-start.5 = (f32[8,40,128]{2,1,0:T(8,128)S(1)}, f32[8,40,128]{2,1,0:T(8,128)}, u32[]{:S(2)}) copy-start(f32[8,40,128]{2,1,0:T(8,128)} %constant.69.clone.b3_ref) | copy-start | bytes 491524
  0.0 55.1 %copy-start.6 = (f32[8,32,128]{2,1,0:T(8,128)S(1)}, f32[8,32,128]{2,1,0:T(8,128)}, u32[]{:S(2)}) copy-start(f32[8,32,128]{2,1,0:T(8,128)} %constant.68.clone.a3_ref) | copy-start | bytes 393220
  0.0 55.1 %copy-start.7 = (f32[32,1024]{1,0:T(8,128)S(1)}, f32[32,1024]{1,0:T(8,128)}, u32[]{:S(2)}) copy-start(f32[32,1024]{1,0:T(8,128)} %constant.67.clone.inv_ref) | copy-start | bytes 393220
  0.0 55.1 %copy-start.1 = (bf16[2,4,256,256]{3,2,1,0:T(8,128)(2,1)S(1)}, bf16[2,4,256,256]{3,2,1,0:T(8,128)(2,1)}, u32[]{:S(2)}) copy-start(bf16[2,4,256,256]{3,2,1,0:T(8,128)(2,1)} %constant.66.clone.ltab_hbm) | copy-start | bytes 3145732
  0.0 55.1 %copy-start.2 = (bf16[2,4,256,256]{3,2,1,0:T(8,128)(2,1)S(1)}, bf16[2,4,256,256]{3,2,1,0:T(8,128)(2,1)}, u32[]{:S(2)}) copy-start(bf16[2,4,256,256]{3,2,1,0:T(8,128)(2,1)} %constant.65.clone.ktab_hbm) | copy-start | bytes 3145732
  0.0 55.1 %copy-start.10 = (s32[192,56]{0,1:T(8,128)S(1)}, s32[192,56]{0,1:T(8,128)}, u32[]{:S(2)}) copy-start(s32[192,56]{0,1:T(8,128)} %param.15) | copy-start | bytes 129028
  0.1 55.1 %copy-start.9 = (s32[192,56]{0,1:T(8,128)S(1)}, s32[192,56]{0,1:T(8,128)}, u32[]{:S(2)}) copy-start(s32[192,56]{0,1:T(8,128)} %param.14) | copy-start | bytes 129028
  0.1 55.1 %copy-start.11 = (s32[96]{0:T(128)S(1)}, s32[96]{0:T(128)}, u32[]{:S(2)}) copy-start(s32[96]{0:T(128)} %shift_ref.1) | copy-start | bytes 1156
  55.1 1.4 %copy-start = (bf16[96,8,1024]{2,1,0:T(8,128)(2,1)S(1)}, bf16[96,8,1024]{2,1,0:T(8,128)(2,1)}, u32[]{:S(2)}) copy-start(bf16[96,8,1024]{2,1,0:T(8,128)(2,1)} %get-tuple-element.11.own.own_hbm) | copy-start | bytes 4718596
  56.6 0.8 copy-start.3
  57.4 0.9 copy-start.4

commit v4 on v3

--- a/solution.py
+++ b/solution.py
@@ -135,47 +135,50 @@
     return both[:rows] + both[rows:] + low
 
 
-GROUP = 16
-
-
-def prep_kernel(orb_ref, pot_ref, own_ref, planes_ref, fold):
-    @pl.when(pl.program_id(0) == 0)
-    def _():
-        fold[0] = folding(0)
-        fold[1] = folding(1)
-        rest = pot_ref[...]
-        planes = []
-        for _ in range(3):
-            top = rest.astype(jnp.bfloat16).astype(jnp.float32)
-            planes.append(top)
-            rest = rest - top
-        x = jnp.concatenate(planes + [jnp.zeros_like(rest)], axis=0).astype(jnp.bfloat16)
+GROUP = 32
+
+
+def prep_kernel(orb_ref, pot_ref, own_ref, planes_ref):
+    fold = [folding(0), folding(1)]
+
+    def some(g, _):
+        x = orb_ref[pl.ds(g * GROUP, GROUP)].astype(jnp.float32)
+        x = x.reshape(GROUP * CX, CROSS).astype(jnp.bfloat16)
         for n in range(4):
             y = jnp.dot(
-                x[:, n * QUAD : (n + 1) * QUAD], fold[n // 2], preferred_element_type=jnp.float32
+                x[:, n * QUAD : (n + 1) * QUAD],
+                fold[n // 2],
+                preferred_element_type=jnp.float32,
             )
             for hz, lanes in enumerate(chunk_home(n)):
-                for p in range(4):
-                    part = y[p * CX : (p + 1) * CX, hz * 128 : hz * 128 + 128]
-                    planes_ref[p // 2, p % 2, :, lanes] = part.astype(jnp.bfloat16)
-
-    x = orb_ref[...].astype(jnp.float32)
-    x = x.reshape(GROUP * CX, CROSS).astype(jnp.bfloat16)
+                part = y[:, hz * 128 : hz * 128 + 128].reshape(GROUP, CX, 128)
+                own_ref[pl.ds(g * GROUP, GROUP), :, lanes] = part.astype(jnp.bfloat16)
+        return 0
+
+    lax.fori_loop(0, NCOL // GROUP, some, 0)
+    rest = pot_ref[...]
+    planes = []
+    for _ in range(3):
+        top = rest.astype(jnp.bfloat16).astype(jnp.float32)
+        planes.append(top)
+        rest = rest - top
+    x = jnp.concatenate(planes + [jnp.zeros_like(rest)], axis=0).astype(jnp.bfloat16)
     for n in range(4):
         y = jnp.dot(
             x[:, n * QUAD : (n + 1) * QUAD], fold[n // 2], preferred_element_type=jnp.float32
         )
         for hz, lanes in enumerate(chunk_home(n)):
-            part = y[:, hz * 128 : hz * 128 + 128].reshape(GROUP, CX, 128)
-            own_ref[:, :, lanes] = part.astype(jnp.bfloat16)
+            for p in range(4):
+                part = y[p * CX : (p + 1) * CX, hz * 128 : hz * 128 + 128]
+                planes_ref[p // 2, p % 2, :, lanes] = part.astype(jnp.bfloat16)
 
 
 def solve_kernel(
     idx_ref, shift_ref, partner_ref, member_ref,
-    own_hbm, win_hbm, pot_ref, potw_ref,
+    own_hbm, win_hbm, pot_hbm, potw_hbm,
     ktab_hbm, ltab_hbm, inv_ref, a3_ref, b3_ref, lx_ref,
     out_ref, table_ref,
-    own_ref, win_ref, ktab_ref, ltab_ref, ktr_ref,
+    own_ref, win_ref, pot_ref, potw_ref, ktab_ref, ltab_ref, ktr_ref,
     wv, pots, acc, stg, home, listed, sems,
 ):
     slab = idx_ref[0]
@@ -188,6 +191,8 @@
         ),
         pltpu.make_async_copy(ltab_hbm, ltab_ref, sems.at[WIDTH + 1]),
         pltpu.make_async_copy(ktab_hbm, ktab_ref, sems.at[WIDTH + 2]),
+        pltpu.make_async_copy(pot_hbm, pot_ref, sems.at[WIDTH + 3]),
+        pltpu.make_async_copy(potw_hbm, potw_ref, sems.at[WIDTH + 4]),
     ]
     for load in loads:
         load.start()
@@ -237,11 +242,6 @@
         f = jnp.float32
         return planes[0, 0].astype(f) + planes[0, 1].astype(f) + planes[1, 0].astype(f)
 
-    pots[lead_rows] = whole(pot_ref)
-    pots[tail_rows] = whole(potw_ref.at[WIDTH - 1])
-    for k in range(1, WIDTH):
-        pots[k * CX : (k + 1) * CX] = whole(potw_ref.at[k - 1])
-
     def widen(rows, source):
         def one(c, _):
             wv[c, rows] = source[c].astype(jnp.float32)
@@ -257,6 +257,12 @@
         widen(rows, win_ref.at[k])
     loads[WIDTH + 1].wait()
     loads[WIDTH + 2].wait()
+    loads[WIDTH + 3].wait()
+    loads[WIDTH + 4].wait()
+    pots[lead_rows] = whole(pot_ref)
+    pots[tail_rows] = whole(potw_ref.at[WIDTH - 1])
+    for k in range(1, WIDTH):
+        pots[k * CX : (k + 1) * CX] = whole(potw_ref.at[k - 1])
     for h in range(2):
         for q in range(4):
             ktr_ref[h, q] = ktab_ref[h, q].astype(jnp.float32).T.astype(jnp.bfloat16)
@@ -558,16 +564,9 @@
             jax.ShapeDtypeStruct((NCOL, CX, CROSS), jnp.bfloat16),
             jax.ShapeDtypeStruct((2, 2, CX, CROSS), jnp.bfloat16),
         ),
-        grid=(NCOL // GROUP,),
-        in_specs=[
-            pl.BlockSpec((GROUP, CX, CROSS), lambda g: (g, 0, 0)),
-            pl.BlockSpec((CX, CROSS), lambda g: (0, 0)),
-        ],
-        out_specs=(
-            pl.BlockSpec((GROUP, CX, CROSS), lambda g: (g, 0, 0)),
-            pl.BlockSpec((2, 2, CX, CROSS), lambda g: (0, 0, 0, 0)),
-        ),
-        scratch_shapes=[pltpu.VMEM((2, QUAD, QUAD), jnp.bfloat16)],
+        in_specs=[vmem] * 2,
+        out_specs=(vmem, vmem),
+        compiler_params=pltpu.CompilerParams(vmem_limit_bytes=16 * 2**20),
         name="prep",
     )(orbitals, potential)
     streams = (WIDTH, PIECES + 1)
@@ -580,7 +579,9 @@
         in_specs=[hbm] * 2,
         out_specs=(hbm, hbm),
         scratch_shapes=[dma(streams)] * 4,
-        compiler_params=pltpu.CompilerParams(collective_id=0, has_side_effects=True),
+        compiler_params=pltpu.CompilerParams(
+            collective_id=0, has_side_effects=True, vmem_limit_bytes=2 * 2**20
+        ),
         name="fetch",
     )(own, pot)
     idx = jnp.stack([slab, core, high])
@@ -590,11 +591,13 @@
             jax.ShapeDtypeStruct((WIDTH + 1, MINE, CX, CROSS), jnp.float32),
             jax.ShapeDtypeStruct((NCOL,), jnp.int32),
         ),
-        in_specs=[smem] * 4 + [hbm] * 2 + [vmem] * 2 + [hbm] * 2 + [vmem] * 4,
+        in_specs=[smem] * 4 + [hbm] * 6 + [vmem] * 4,
         out_specs=(vmem, smem),
         scratch_shapes=[
             pltpu.VMEM((NCOL, CX, CROSS), jnp.bfloat16),
             pltpu.VMEM((WIDTH, NCOL, CX, CROSS), jnp.bfloat16),
+            pltpu.VMEM((2, 2, CX, CROSS), jnp.bfloat16),
+            pltpu.VMEM((WIDTH, 2, 2, CX, CROSS), jnp.bfloat16),
         ]
         + [pltpu.VMEM((2, 4, QUAD, QUAD), jnp.bfloat16)] * 3
         + [
@@ -605,8 +608,8 @@
             pltpu.SMEM((32,), jnp.int32),
         ]
         + [pltpu.SMEM((SLOTS + BATCH,), jnp.int32)]
-        + [dma((WIDTH + 3,))],
-        compiler_params=pltpu.CompilerParams(vmem_limit_bytes=44 * 2**20),
+        + [dma((WIDTH + 5,))],
+        compiler_params=pltpu.CompilerParams(vmem_limit_bytes=40 * 2**20),
         name="solve",
     )(idx, box_shift, pair_partner.T, pair_member.T, own, win, pot, potw, ktab, ltab, inv, a3, b3, lx)
     piece = (MINE, CX, CROSS)

time: 115 us -> 109 us (0.948); the launches traced: 113 us -> 110 us
  Pallas kernels: 108 us -> 106 us
    pallas_call x1, Pallas kernels: 5.52 us -> 1.16 us  [body(): pl.pallas_call(prep_kernel, out_shape=(jax.ShapeDtypeStruct((NCOL, CX, CR...]
    pallas_call x1, Pallas kernels: 13.6 us -> 16.1 us  [body(): pl.pallas_call(solve_kernel, out_shape=(jax.ShapeDtypeStruct((WIDTH + 1,...]
    unnamed x25 -> x23, local copies, waits for them, and re-layouts: 4.9 us -> 3.87 us
where the time goes in v4:
time: 109 us; the launch traced here: 110 us
  Pallas kernels  106 us (97%)
  local copies, waits for them, and re-layouts  3.87 us (4%)
    pallas_call x1, Pallas kernels, body(): pl.pallas_call(fetch_kernel, out_shape=(jax.ShapeDtypeStruct((WIDTH, NCOL...  48.8 us
    pallas_call x1, Pallas kernels, body(): pl.pallas_call(spread_kernel, out_shape=jax.ShapeDtypeStruct((NCOL, CX, C...  39.5 us
    pallas_call x1, Pallas kernels, body(): pl.pallas_call(solve_kernel, out_shape=(jax.ShapeDtypeStruct((WIDTH + 1,...  16.1 us
    unnamed x23, local copies, waits for them, and re-layouts  3.87 us

profile of v4, /device:TPU:1, one launch (start us, length us, event | category | flops | bytes accessed | tf_op | source)
XLA Modules:
  0.0 109.7 jit_solution(15575572207302363303)
XLA Ops:
  0.0 0.0 copy-start.6
  0.0 0.0 copy-start.10
  0.0 0.1 pad_add_fusion.idx_ref
  0.1 0.0 copy-start
  0.1 1.4 %copy-done = bf16[96,8,1024]{2,1,0:T(8,128)(2,1)S(1)} copy-done((bf16[96,8,1024]{2,1,0:T(8,128)(2,1)S(1)}, bf16[96,8,1024]{2,1,0:T(8,128)(2,1)}, u32[]{:S(2)}) %copy-start) | copy-done | bytes 1572888
  1.5 0.0 copy-start.9
  1.5 0.8 copy-done.9
  2.2 0.0 copy-start.1
  2.3 0.0 copy-start.2
  2.3 0.0 copy-start.3
  2.3 0.0 copy-start.4
  2.3 0.0 copy-start.5
  2.3 0.0 copy-start.7
  2.3 0.0 copy-start.8
  2.3 1.2 %prep.1 = (bf16[96,8,1024]{2,1,0:T(8,128)(2,1)S(1)}, bf16[2,2,8,1024]{3,2,1,0:T(8,128)(2,1)S(1)}) custom-call(bf16[96,8,1024]{2,1,0:T(8,128)(2,1)S(1)} %copy-done, f32[8,1024]{1,0:T(8,128)S(1)} %copy-done.9), custom_call_target="tpu_custom_call" | custom-call | tf_op jit(solution)/shard_map/prep/pallas_call | solution.py:561
  3.5 48.8 %fetch.1 = (bf16[4,96,8,1024]{3,2,1,0:T(8,128)(2,1)S(1)}, bf16[4,2,2,8,1024]{4,3,2,1,0:T(8,128)(2,1)S(1)}) custom-call(bf16[96,8,1024]{2,1,0:T(8,128)(2,1)S(1)} %get-tuple-element.11.own.own_hbm, bf16[2,2,8,1024]{3,2,1,0:T(8,128)(2,1)S(1)} %get-tuple-element.12.pot.pot_hbm), custom_call_target="tpu_custom_call" | custom-call | tf_op jit(solution)/shard_map/fetch/pallas_call | solution.py:573
  52.3 0.0 copy-done.6
  52.3 0.0 copy-done.10
  52.3 0.0 copy-done.1
  52.3 0.0 copy-done.2
  52.3 0.0 copy-done.3
  52.3 0.0 copy-done.4
  52.4 0.0 copy-done.5
  52.4 0.0 copy-done.7
  52.4 0.0 copy-done.8
  52.4 16.1 %solve.1 = (f32[5,12,8,1024]{3,2,1,0:T(8,128)S(1)}, s32[96]{0:T(128)S(1)}) custom-call(s32[3]{0:T(128)S(1)} %pad_add_fusion.idx_ref, s32[96]{0:T(128)S(1)} %copy-done.10, s32[56,192]{1,0:T(8,128)S(1)} %bitcast.5, s32[56,192]{1,0:T(8,128)S(1)} %bitcast.6, bf16[96,8,1024]{2,1,0:T(8,128)(2,1)S(1)} %get-tuple-element.11.own.own_hbm, ...), custom_call_target="tpu_custom_call" | custom-call | tf_op jit(solution)/shard_map/solve/pallas_call | solution.py:588
  68.5 39.5 %spread.1 = f32[96,8,1024]{2,1,0:T(8,128)S(1)} custom-call(s32[96]{0:T(128)S(1)} %get-tuple-element.15.table_ref, f32[5,12,8,1024]{3,2,1,0:T(8,128)S(1)} %get-tuple-element.16.boxes), custom_call_target="tpu_custom_call" | custom-call | tf_op jit(solution)/shard_map/spread/pallas_call | solution.py:617
  108.0 1.7 %copy.13 = f32[96,8,1024]{2,1,0:T(8,128)} copy(f32[96,8,1024]{2,1,0:T(8,128)S(1)} %spread.1) | data formatting | bytes 6291456
Async XLA Ops:
  0.0 52.3 %copy-start.6 = (bf16[8,40,128]{2,1,0:T(8,128)(2,1)S(1)}, bf16[8,40,128]{2,1,0:T(8,128)(2,1)}, u32[]{:S(2)}) copy-start(bf16[8,40,128]{2,1,0:T(8,128)(2,1)} %constant.70.clone.lx_ref) | copy-start | bytes 245764
  0.0 52.3 %copy-start.10 = (s32[96]{0:T(128)S(1)}, s32[96]{0:T(128)}, u32[]{:S(2)}) copy-start(s32[96]{0:T(128)} %shift_ref.1) | copy-start | bytes 1156
  0.1 1.4 %copy-start = (bf16[96,8,1024]{2,1,0:T(8,128)(2,1)S(1)}, bf16[96,8,1024]{2,1,0:T(8,128)(2,1)}, u32[]{:S(2)}) copy-start(bf16[96,8,1024]{2,1,0:T(8,128)(2,1)} %orb_ref.1) | copy-start | bytes 4718596
  1.5 0.8 copy-start.9
  2.2 50.1 %copy-start.1 = (bf16[2,4,256,256]{3,2,1,0:T(8,128)(2,1)S(1)}, bf16[2,4,256,256]{3,2,1,0:T(8,128)(2,1)}, u32[]{:S(2)}) copy-start(bf16[2,4,256,256]{3,2,1,0:T(8,128)(2,1)} %constant.66.clone.ltab_hbm) | copy-start | bytes 3145732
  2.3 50.1 %copy-start.2 = (bf16[2,4,256,256]{3,2,1,0:T(8,128)(2,1)S(1)}, bf16[2,4,256,256]{3,2,1,0:T(8,128)(2,1)}, u32[]{:S(2)}) copy-start(bf16[2,4,256,256]{3,2,1,0:T(8,128)(2,1)} %constant.65.clone.ktab_hbm) | copy-start | bytes 3145732
  2.3 50.1 %copy-start.3 = (f32[8,40,128]{2,1,0:T(8,128)S(1)}, f32[8,40,128]{2,1,0:T(8,128)}, u32[]{:S(2)}) copy-start(f32[8,40,128]{2,1,0:T(8,128)} %constant.69.clone.b3_ref) | copy-start | bytes 491524
  2.3 50.1 %copy-start.4 = (f32[8,32,128]{2,1,0:T(8,128)S(1)}, f32[8,32,128]{2,1,0:T(8,128)}, u32[]{:S(2)}) copy-start(f32[8,32,128]{2,1,0:T(8,128)} %constant.68.clone.a3_ref) | copy-start | bytes 393220
  2.3 50.1 %copy-start.5 = (f32[32,1024]{1,0:T(8,128)S(1)}, f32[32,1024]{1,0:T(8,128)}, u32[]{:S(2)}) copy-start(f32[32,1024]{1,0:T(8,128)} %constant.67.clone.inv_ref) | copy-start | bytes 393220
  2.3 50.1 %copy-start.7 = (s32[192,56]{0,1:T(8,128)S(1)}, s32[192,56]{0,1:T(8,128)}, u32[]{:S(2)}) copy-start(s32[192,56]{0,1:T(8,128)} %param.14) | copy-start | bytes 129028
  2.3 50.1 %copy-start.8 = (s32[192,56]{0,1:T(8,128)S(1)}, s32[192,56]{0,1:T(8,128)}, u32[]{:S(2)}) copy-start(s32[192,56]{0,1:T(8,128)} %param.15) | copy-start | bytes 129028
